TPU v7x, 768 devices: a whole 4x8x12 slice. The times are simulated.
768 devices in a mesh: samp: 64 (over y, x, core), sx: 6 (over z_lo), sy: 2 (over z_hi).
Axes of the slice: x: 4, y: 8, z: 12 (z_hi: 2, z_lo: 6; z = z_hi * 6 + z_lo), core: 2. Of those that a mesh axis runs over, the one named last changes fastest.
Arguments:
- volume: bfloat16 [64, 32, 12, 16, 128], P('samp', None, 'sx', 'sy'), may hold values from -6 to 6
- kernel: bfloat16 [64, 32, 3, 3, 3], replicated, may hold values from -0.21875 to 0.21875
- bias: float32 [64], replicated, may hold values from -4 to 4
- upstream: bfloat16 [64, 64, 12, 16, 128], P('samp', None, 'sx', 'sy'), may hold values from -6 to 6
Outputs:
- activated: bfloat16 [64, 64, 12, 16, 128], P('samp', None, 'sx', 'sy')
- input_grad: bfloat16 [64, 32, 12, 16, 128], P('samp', None, 'sx', 'sy')
- filter_grad: float32 [64, 32, 3, 3, 3], replicated
- bias_grad: float32 [64], replicated
All inputs are finite; a program needn't handle non-finite values.
Results may differ from a plain program's by a relative error of at most 0.0065.
Values may be sent and summed in bfloat16 or wider, within the bound.
No kernel may reach another device: no remote copies, remote signals or barrier semaphores. Data moves between devices by JAX's collectives and lax.ppermute only.
A program may use at most 64 MiB of HBM per device.

v0:
```python
import jax
import jax.numpy as jnp
from jax import lax
from jax.sharding import PartitionSpec as P


def extended(shard, sides, width):
    for axis, dim in sides:
        size, length = (lax.axis_size(axis), shard.shape[dim])
        up = [(i, (i + 1) % size) for i in range(size - 1)]
        down = [(j, i) for i, j in up]
        last = lax.slice_in_dim(shard, length - width, length, axis=dim)
        initial = lax.slice_in_dim(shard, 0, width, axis=dim)
        before = lax.ppermute(last, axis, up)
        after = lax.ppermute(initial, axis, down)
        shard = jnp.concatenate([before, shard, after], axis=dim)
    return shard


def in_blocks(shard, dim, size):
    before, after = (shard.shape[:dim], shard.shape[dim + 1 :])
    return jnp.moveaxis(shard.reshape(*before, size, -1, *after), dim, 0)


def sent_and_summed(shard, axis, dim):
    size = lax.axis_size(axis)
    blocks = lax.all_to_all(in_blocks(shard, dim, size), axis, 0, 0, tiled=True)
    return jnp.sum(blocks, axis=0)


def sent_to_all(shard, axis):
    copies = jnp.broadcast_to(shard, (lax.axis_size(axis), *shard.shape))
    return lax.all_to_all(copies, axis, split_axis=0, concat_axis=0, tiled=True)


def taken_together(shard, axis):
    return sent_to_all(shard, axis).sum(axis=0)


def in_order(blocks, dim):
    lengths = list(blocks.shape[1:])
    lengths[dim] *= blocks.shape[0]
    return jnp.moveaxis(blocks, 0, dim).reshape(lengths)


def gathered_copies(shard, axis, dim):
    return in_order(sent_to_all(shard, axis), dim)


def conv_forward(padded, kernel):
    return lax.conv_general_dilated(
        padded,
        kernel,
        (1, 1, 1),
        ((0, 0), (0, 0), (1, 1)),
        dimension_numbers=("NCDHW", "OIDHW", "NCDHW"),
        preferred_element_type=jnp.float32,
    )


def conv_backward(padded, kernel):
    flipped = kernel[:, :, ::-1, ::-1, ::-1]
    return lax.conv_general_dilated(
        padded,
        flipped,
        (1, 1, 1),
        ((0, 0), (0, 0), (1, 1)),
        dimension_numbers=("NCDHW", "IODHW", "NCDHW"),
        preferred_element_type=jnp.float32,
    )


def filter_terms(padded, delta):
    return lax.conv_general_dilated(
        padded,
        delta,
        (1, 1, 1),
        ((0, 0), (0, 0), (1, 1)),
        dimension_numbers=("CNDHW", "IODHW", "CNDHW"),
        preferred_element_type=jnp.float32,
    )


def slope_of(pre):
    return 0.3 + 0.7 * jax.nn.sigmoid(pre)


def per_device(volume, kernel, bias, upstream):
    samples, rows, cols, depth = (
        volume.shape[0],
        volume.shape[2],
        volume.shape[3],
        volume.shape[4],
    )
    bias_wide = bias[None, :, None, None, None]
    padded = extended(volume, (("sx", 2), ("sy", 3)), 1)
    pre = conv_forward(padded, kernel) + bias_wide
    delta = (upstream.astype(jnp.float32) * slope_of(pre)).astype(jnp.bfloat16)
    delta_pad = extended(delta, (("sx", 2), ("sy", 3)), 1)
    activated = (0.3 * pre + 0.7 * jax.nn.softplus(pre)).astype(jnp.bfloat16)
    input_grad = conv_backward(delta_pad, kernel).astype(jnp.bfloat16)
    wgrad = filter_terms(padded, delta)
    bgrad = jnp.sum(delta.astype(jnp.float32), axis=(0, 2, 3, 4))
    groups = lax.axis_size("sx") * lax.axis_size("sy")
    whole = lax.axis_size("samp") * samples * groups * rows * cols * depth
    norm = 1.0 / jnp.sqrt(jnp.float32(whole))
    joined = jnp.concatenate([wgrad.reshape(-1), bgrad])
    count = joined.shape[0]
    padded_len = (count + groups - 1) // groups * groups
    joined = jnp.pad(joined, (0, padded_len - count))
    share = sent_and_summed(joined, ("sx", "sy"), 0)
    share = taken_together(share, "samp")
    summed = gathered_copies(share, ("sx", "sy"), 0)
    wsum = summed[: wgrad.size].reshape(wgrad.shape)
    bsum = summed[wgrad.size : count]
    return (activated, input_grad, wsum * norm, bsum * norm)


def solution(mesh):
    in_specs = (P("samp", None, "sx", "sy", None), P(), P(), P("samp", None, "sx", "sy", None))
    out_specs = (P("samp", None, "sx", "sy", None), P("samp", None, "sx", "sy", None), P(), P())
    return jax.shard_map(
        per_device, mesh=mesh, in_specs=in_specs, out_specs=out_specs, check_vma=False
    )
```

profile of v0, /device:TPU:2, one launch (start us, length us, event | category | flops | bytes accessed | tf_op | source)
XLA Modules:
  0.0 235.1 jit_solution(7462722179932837052)
XLA Ops:
  0.6 0.9 fusion.47
  1.6 4.3 %collective-permute-start = (bf16[1,32,1,8,128]{4,3,2,1,0:T(8,128)(2,1)S(1)}, bf16[1,32,1,8,128]{4,3,2,1,0:T(8,128)(2,1)S(1)}, u32[]{:S(2)}, u32[]{:S(2)}) collective-permute-start(bf16[1,32,1,8,128]{4,3,2,1,0:T(8,128)(2,1)S(1)} %get-tuple-element.30), channel_id=1, source_target_pairs={{0,2},{2,4},{4,6},{6,8},{8,10},{1,3},{3,5},{5,7},{7,9},{9,11},{12,... | collective-permute-start | bytes 196616 | tf_op jit(solution)/shard_map/ppermute | solution.py:14
  5.9 1.3 collective-permute-start.1
  7.2 0.6 collective-permute-done
  7.7 4.6 %collective-permute-done.1 = bf16[1,32,1,8,128]{4,3,2,1,0:T(8,128)(2,1)S(1)} collective-permute-done((bf16[1,32,1,8,128]{4,3,2,1,0:T(8,128)(2,1)S(1)}, bf16[1,32,1,8,128]{4,3,2,1,0:T(8,128)(2,1)S(1)}, u32[]{:S(2)}, u32[]{:S(2)}) %collective-permute-start.1) | collective-permute-done | bytes 65568 | tf_op jit(solution)/shard_map/ppermute | solution.py:15
  12.4 1.0 pad_maximum_fusion.2
  13.4 1.2 copy.75
  14.6 1.2 fusion.44
  15.8 14.5 %collective-permute-start.2 = (bf16[1,32,4,1,128]{1,0,4,3,2:T(2,128)(2,1)}, bf16[1,32,4,1,128]{1,0,4,3,2:T(2,128)(2,1)S(1)}, u32[]{:S(2)}, u32[]{:S(2)}) collective-permute-start(bf16[1,32,4,1,128]{1,0,4,3,2:T(2,128)(2,1)} %get-tuple-element.22), channel_id=1, source_target_pairs={{0,1},{2,3},{4,5},{6,7},{8,9},{10,11},{12,13},{14,15},{16,17},{18,... | collective-permute-start | bytes 98312 | tf_op jit(solution)/shard_map/ppermute | solution.py:14
  30.3 1.3 collective-permute-start.3
  31.6 1.2 copy.83
  32.8 1.9 collective-permute-done.2
  34.7 20.2 %collective-permute-done.3 = bf16[1,32,4,1,128]{1,0,4,3,2:T(2,128)(2,1)S(1)} collective-permute-done((bf16[1,32,4,1,128]{1,0,4,3,2:T(2,128)(2,1)S(1)}, bf16[1,32,4,1,128]{1,0,4,3,2:T(2,128)(2,1)S(1)}, u32[]{:S(2)}, u32[]{:S(2)}) %collective-permute-start.3) | collective-permute-done | bytes 32800 | tf_op jit(solution)/shard_map/ppermute | solution.py:15
  54.9 10.6 %pad_maximum_fusion = bf16[1,32,4,10,128]{1,0,4,3,2:T(2,128)(2,1)} fusion(bf16[1,32,4,1,128]{1,0,4,3,2:T(2,128)(2,1)S(1)} %collective-permute-done.3, bf16[1,32,4,8,128]{1,0,4,3,2:T(2,128)(2,1)S(1)} %copy.75, bf16[1,32,4,1,128]{1,0,4,3,2:T(2,128)(2,1)S(1)} %collective-permute-done.2), kind=kLoop, calls=%fused_computation.5 | loop fusion | flops 327680 | bytes 655360 | tf_op jit(solution)/shard_map/concatenate | solution.py:16
  65.5 4.7 %copy.78 = bf16[1,32,4,10,128]{4,1,3,2,0:T(8,128)(2,1)S(1)} copy(bf16[1,32,4,10,128]{1,0,4,3,2:T(2,128)(2,1)} %pad_maximum_fusion) | data formatting | bytes 655360 | tf_op jit(solution)/shard_map/concatenate | solution.py:16
  70.2 1.0 copy.99
  71.2 0.7 pad.5.clone
  71.9 0.2 copy.81
  72.2 0.4 copy-done.6
  72.6 0.0 copy-done.7
  72.6 3.4 %multiply_add_fusion = (f32[2,8,8,17,64]{4,2,3,1,0:T(8,128)S(1)}, bf16[2,8,8,17,64]{4,2,3,1,0:T(8,128)(2,1)}) fusion(f32[64]{0:T(128)S(1)} %copy-done.6, bf16[64,32,3,3,3]{0,1,4,3,2:T(8,128)(2,1)S(1)} %copy-done, bf16[32,4,10,1,7,2]{0,4,5,2,1,3:T(8,128)(2,1)S(1)} %slice.47, bf16[32,4,10,1,8,17]{0,4,5,2,1,3:T(8,128)(2,1)S(1)} %copy.81, ...), kind=kOutput, calls=%fused_computation.25 | convolution fusion | flops 244183040 | bytes 1330568 | tf_op jit(solution)/shard_map/conv_general_dilated | solution.py:51
  76.0 0.2 copy.84
  76.3 0.8 copy-done.2
  77.1 0.8 convert_reduce_fusion
  77.9 0.1 copy-done.1
  78.0 15.1 %fusion.33 = f32[64,32,3,3,3]{0,1,4,3,2:T(8,128)S(1)} fusion(bf16[1,32,4,10,128]{1,0,4,3,2:T(2,128)(2,1)S(1)} %copy-done.1, bf16[1,64,2,8,128]{1,3,4,2,0:T(8,128)(2,1)S(1)} %get-tuple-element.21), kind=kOutput, calls=%fused_computation.31 | convolution fusion | flops 225312768 | bytes 811008 | tf_op jit(solution)/shard_map/conv_general_dilated | solution.py:74
  93.0 12.1 %copy.93 = f32[64,32,3,3,3]{4,3,2,1,0:T(4,128)} copy(f32[64,32,3,3,3]{0,1,4,3,2:T(8,128)S(1)} %fusion.33) | data formatting | bytes 442368 | tf_op jit(solution)/shard_map/conv_general_dilated | solution.py:74
  105.2 10.4 %reshape.33 = f32[55296]{0:T(1024)S(1)} reshape(f32[64,32,3,3,3]{4,3,2,1,0:T(4,128)} %copy.93) | data formatting | bytes 442368 | tf_op jit(solution)/shard_map/reshape | solution.py:107
  115.6 0.3 all_to_all.14
  115.9 19.6 %all_to_all.21 = f32[12,1,4614]{2,1,0:T(1,128)S(1)} all-to-all(f32[12,1,4614]{2,1,0:T(1,128)S(1)} %all_to_all.14), channel_id=1, replica_groups=mesh['samp'=64,'sx'=6,'sy'=2] {'sx','sy'}, dimensions={0} | all-to-all | bytes 442944 | tf_op jit(solution)/shard_map/all_to_all | solution.py:27
  135.5 0.2 reduce_sum.28
  135.7 1.7 broadcast_in_dim.7
  137.4 10.8 %all-to-all-start.1 = ((f32[64,1,4614]{2,1,0:T(1,128)}), f32[64,1,4614]{2,1,0:T(1,128)S(1)}, u32[]{:S(2)}, u32[]{:S(2)}) async-start(f32[64,1,4614]{2,1,0:T(1,128)} %broadcast_in_dim.7), calls=%async_computation.1 | async-start | bytes 2424832 | tf_op jit(solution)/shard_map/all_to_all | solution.py:33
  148.2 1.8 collective-permute-start.4
  150.0 1.3 collective-permute-start.5
  151.3 0.1 copy.82
  151.4 4.4 %collective-permute-done.4 = bf16[1,64,1,8,128]{1,3,4,2,0:T(8,128)(2,1)S(1)} collective-permute-done((bf16[1,64,1,8,128]{1,3,4,2,0:T(8,128)(2,1)S(1)}, bf16[1,64,1,8,128]{1,3,4,2,0:T(8,128)(2,1)S(1)}, u32[]{:S(2)}, u32[]{:S(2)}) %collective-permute-start.4) | collective-permute-done | bytes 131104 | tf_op jit(solution)/shard_map/ppermute | solution.py:14
  155.8 4.1 %collective-permute-done.5 = bf16[1,64,1,8,128]{1,3,4,2,0:T(8,128)(2,1)S(1)} collective-permute-done((bf16[1,64,1,8,128]{1,3,4,2,0:T(8,128)(2,1)S(1)}, bf16[1,64,1,8,128]{1,3,4,2,0:T(8,128)(2,1)S(1)}, u32[]{:S(2)}, u32[]{:S(2)}) %collective-permute-start.5) | collective-permute-done | bytes 131104 | tf_op jit(solution)/shard_map/ppermute | solution.py:15
  159.9 0.2 pad_maximum_fusion.1
  160.2 1.1 fusion.45
  161.3 6.0 %collective-permute-start.6 = (bf16[1,64,4,1,128]{1,3,4,2,0:T(2,128)(2,1)}, bf16[1,64,4,1,128]{1,3,4,2,0:T(2,128)(2,1)S(1)}, u32[]{:S(2)}, u32[]{:S(2)}) collective-permute-start(bf16[1,64,4,1,128]{1,3,4,2,0:T(2,128)(2,1)} %get-tuple-element.26), channel_id=1, source_target_pairs={{0,1},{2,3},{4,5},{6,7},{8,9},{10,11},{12,13},{14,15},{16,17},{18,... | collective-permute-start | bytes 196616 | tf_op jit(solution)/shard_map/ppermute | solution.py:14
  167.3 1.3 collective-permute-start.7
  168.6 1.1 copy.95
  169.8 0.6 copy.86
  170.4 2.1 collective-permute-done.6
  172.6 0.1 copy.85
  172.7 18.9 %collective-permute-done.7 = bf16[1,64,4,1,128]{1,3,4,2,0:T(2,128)(2,1)S(1)} collective-permute-done((bf16[1,64,4,1,128]{1,3,4,2,0:T(2,128)(2,1)}, bf16[1,64,4,1,128]{1,3,4,2,0:T(2,128)(2,1)S(1)}, u32[]{:S(2)}, u32[]{:S(2)}) %collective-permute-start.7) | collective-permute-done | bytes 65568 | tf_op jit(solution)/shard_map/ppermute | solution.py:15
  191.6 0.1 copy.87
  191.7 0.1 maximum_bitcast_fusion
  191.8 1.8 copy.100
  193.7 0.7 pad.7.clone
  194.4 0.2 copy.90
  194.6 0.9 reduce_sum.29
  195.5 0.8 broadcast_in_dim.8
  196.3 5.1 %all-to-all-start.2 = ((f32[12,1,4614]{2,1,0:T(1,128)}), f32[12,1,4614]{2,1,0:T(1,128)S(1)}, u32[]{:S(2)}, u32[]{:S(2)}) async-start(f32[12,1,4614]{2,1,0:T(1,128)} %broadcast_in_dim.8), calls=%async_computation.2 | async-start | bytes 454656 | tf_op jit(solution)/shard_map/all_to_all | solution.py:33
  201.4 4.0 %fusion.25 = bf16[2,8,8,17,32]{4,2,3,1,0:T(8,128)(2,1)S(1)} fusion(bf16[64,32,3,3,3]{0,1,4,3,2:T(8,128)(2,1)S(1)} %copy-done, bf16[64,4,10,1,7,2]{0,4,5,2,1,3:T(8,128)(2,1)S(1)} %slice.54, bf16[64,4,10,1,8,17]{0,4,5,2,1,3:T(8,128)(2,1)S(1)} %copy.90, pred[8,17]{0,1:T(8,128)(4,1)S(1)} %copy-done.8), kind=kOutput, calls=%fused_computation.21 | convolution fusion | flops 243122176 | bytes 1017992 | tf_op jit(solution)/shard_map/conv_general_dilated | solution.py:63
  205.4 0.1 copy.91
  205.6 1.0 copy.96
  206.6 6.8 %all-to-all-done.2 = f32[12,1,4614]{2,1,0:T(1,128)S(1)} async-done(((f32[12,1,4614]{2,1,0:T(1,128)}), f32[12,1,4614]{2,1,0:T(1,128)S(1)}, u32[]{:S(2)}, u32[]{:S(2)}) %all-to-all-start.2) | async-done | bytes 221504 | tf_op jit(solution)/shard_map/all_to_all | solution.py:33
  213.4 0.5 reduce.2
  214.0 0.1 reshape.34
  214.1 0.5 slice_multiply_fusion.1
  214.7 8.3 %mul.33 = f32[64,32,3,3,3]{4,3,2,1,0:T(4,128)} reshape(f32[55296]{0:T(1024)S(1)} %slice_multiply_fusion) | data formatting | bytes 442368 | tf_op jit(solution)/shard_map/mul | solution.py:116
  223.0 11.7 %copy.97 = f32[64,32,3,3,3]{0,1,4,3,2:T(8,128)} copy(f32[64,32,3,3,3]{4,3,2,1,0:T(4,128)} %mul.33) | data formatting | bytes 442368
  (22 shorter events, 0.3 us)
Async XLA Ops:
  0.6 71.5 %copy-start = (bf16[64,32,3,3,3]{0,1,4,3,2:T(8,128)(2,1)S(1)}, bf16[64,32,3,3,3]{0,1,4,3,2:T(8,128)(2,1)}, u32[]{:S(2)}) copy-start(bf16[64,32,3,3,3]{0,1,4,3,2:T(8,128)(2,1)} %param.5) | copy-start | bytes 331780
  1.6 6.2 %collective-permute-start = (bf16[1,32,1,8,128]{4,3,2,1,0:T(8,128)(2,1)S(1)}, bf16[1,32,1,8,128]{4,3,2,1,0:T(8,128)(2,1)S(1)}, u32[]{:S(2)}, u32[]{:S(2)}) collective-permute-start(bf16[1,32,1,8,128]{4,3,2,1,0:T(8,128)(2,1)S(1)} %get-tuple-element.30), channel_id=1, source_target_pairs={{0,2},{2,4},{4,6},{6,8},{8,10},{1,3},{3,5},{5,7},{7,9},{9,11},{12,... | collective-permute-start | bytes 196616 | tf_op jit(solution)/shard_map/ppermute | solution.py:14
  5.9 6.5 %collective-permute-start.1 = (bf16[1,32,1,8,128]{4,3,2,1,0:T(8,128)(2,1)S(1)}, bf16[1,32,1,8,128]{4,3,2,1,0:T(8,128)(2,1)S(1)}, u32[]{:S(2)}, u32[]{:S(2)}) collective-permute-start(bf16[1,32,1,8,128]{4,3,2,1,0:T(8,128)(2,1)S(1)} %get-tuple-element.31), channel_id=1, source_target_pairs={{2,0},{4,2},{6,4},{8,6},{10,8},{3,1},{5,3},{7,5},{9,7},{11,9},{14,... | collective-permute-start | bytes 196616 | tf_op jit(solution)/shard_map/ppermute | solution.py:15
  13.3 18.3 %copy-start.4 = (bf16[1,64,2,8,128]{4,3,2,1,0:T(8,128)(2,1)S(1)}, bf16[1,64,2,8,128]{4,3,2,1,0:T(8,128)(2,1)}, u32[]{:S(2)}) copy-start(bf16[1,64,2,8,128]{4,3,2,1,0:T(8,128)(2,1)} %param.7) | copy-start | bytes 786436
  15.8 18.9 %collective-permute-start.2 = (bf16[1,32,4,1,128]{1,0,4,3,2:T(2,128)(2,1)}, bf16[1,32,4,1,128]{1,0,4,3,2:T(2,128)(2,1)S(1)}, u32[]{:S(2)}, u32[]{:S(2)}) collective-permute-start(bf16[1,32,4,1,128]{1,0,4,3,2:T(2,128)(2,1)} %get-tuple-element.22), channel_id=1, source_target_pairs={{0,1},{2,3},{4,5},{6,7},{8,9},{10,11},{12,13},{14,15},{16,17},{18,... | collective-permute-start | bytes 98312 | tf_op jit(solution)/shard_map/ppermute | solution.py:14
  30.3 24.6 %collective-permute-start.3 = (bf16[1,32,4,1,128]{1,0,4,3,2:T(2,128)(2,1)S(1)}, bf16[1,32,4,1,128]{1,0,4,3,2:T(2,128)(2,1)S(1)}, u32[]{:S(2)}, u32[]{:S(2)}) collective-permute-start(bf16[1,32,4,1,128]{1,0,4,3,2:T(2,128)(2,1)S(1)} %get-tuple-element.23), channel_id=1, source_target_pairs={{1,0},{3,2},{5,4},{7,6},{9,8},{11,10},{13,12},{15,14},{17,16},{19,... | collective-permute-start | bytes 98312 | tf_op jit(solution)/shard_map/ppermute | solution.py:15
  71.9 0.7 copy-start.6
  71.9 0.7 copy-start.7
  76.0 1.0 copy-start.2
  76.0 1.9 copy-start.1
  105.2 10.4 %copy-start.5 = (f32[64]{0:T(128)S(1)}, f32[64]{0:T(128)}, u32[]{:S(2)}) copy-start(f32[64]{0:T(128)} %get-tuple-element.20) | copy-start | bytes 772
  137.4 13.9 %copy-start.3 = (bf16[2,8,8,17,64]{4,2,3,1,0:T(8,128)(2,1)S(1)}, bf16[2,8,8,17,64]{4,2,3,1,0:T(8,128)(2,1)}, u32[]{:S(2)}) copy-start(bf16[2,8,8,17,64]{4,2,3,1,0:T(8,128)(2,1)} %get-tuple-element.25) | copy-start | bytes 835588
  137.4 57.3 %all-to-all-start.1 = ((f32[64,1,4614]{2,1,0:T(1,128)}), f32[64,1,4614]{2,1,0:T(1,128)S(1)}, u32[]{:S(2)}, u32[]{:S(2)}) async-start(f32[64,1,4614]{2,1,0:T(1,128)} %broadcast_in_dim.7), calls=%async_computation.1 | async-start | bytes 2424832 | tf_op jit(solution)/shard_map/all_to_all | solution.py:33
  148.2 7.6 %collective-permute-start.4 = (bf16[1,64,1,8,128]{1,3,4,2,0:T(8,128)(2,1)S(1)}, bf16[1,64,1,8,128]{1,3,4,2,0:T(8,128)(2,1)S(1)}, u32[]{:S(2)}, u32[]{:S(2)}) collective-permute-start(bf16[1,64,1,8,128]{1,3,4,2,0:T(8,128)(2,1)S(1)} %get-tuple-element.28), channel_id=1, source_target_pairs={{0,2},{2,4},{4,6},{6,8},{8,10},{1,3},{3,5},{5,7},{7,9},{9,11},{12,... | collective-permute-start | bytes 393224 | tf_op jit(solution)/shard_map/ppermute | solution.py:14
  150.0 9.9 %collective-permute-start.5 = (bf16[1,64,1,8,128]{1,3,4,2,0:T(8,128)(2,1)S(1)}, bf16[1,64,1,8,128]{1,3,4,2,0:T(8,128)(2,1)S(1)}, u32[]{:S(2)}, u32[]{:S(2)}) collective-permute-start(bf16[1,64,1,8,128]{1,3,4,2,0:T(8,128)(2,1)S(1)} %get-tuple-element.29), channel_id=1, source_target_pairs={{2,0},{4,2},{6,4},{8,6},{10,8},{3,1},{5,3},{7,5},{9,7},{11,9},{14,... | collective-permute-start | bytes 393224 | tf_op jit(solution)/shard_map/ppermute | solution.py:15
  161.3 11.2 %collective-permute-start.6 = (bf16[1,64,4,1,128]{1,3,4,2,0:T(2,128)(2,1)}, bf16[1,64,4,1,128]{1,3,4,2,0:T(2,128)(2,1)S(1)}, u32[]{:S(2)}, u32[]{:S(2)}) collective-permute-start(bf16[1,64,4,1,128]{1,3,4,2,0:T(2,128)(2,1)} %get-tuple-element.26), channel_id=1, source_target_pairs={{0,1},{2,3},{4,5},{6,7},{8,9},{10,11},{12,13},{14,15},{16,17},{18,... | collective-permute-start | bytes 196616 | tf_op jit(solution)/shard_map/ppermute | solution.py:14
  167.3 24.3 %collective-permute-start.7 = (bf16[1,64,4,1,128]{1,3,4,2,0:T(2,128)(2,1)}, bf16[1,64,4,1,128]{1,3,4,2,0:T(2,128)(2,1)S(1)}, u32[]{:S(2)}, u32[]{:S(2)}) collective-permute-start(bf16[1,64,4,1,128]{1,3,4,2,0:T(2,128)(2,1)} %get-tuple-element.27), channel_id=1, source_target_pairs={{1,0},{3,2},{5,4},{7,6},{9,8},{11,10},{13,12},{15,14},{17,16},{19,... | collective-permute-start | bytes 196616 | tf_op jit(solution)/shard_map/ppermute | solution.py:15
  194.6 6.8 %copy-start.8 = (pred[8,17]{0,1:T(8,128)(4,1)S(1)}, pred[8,17]{0,1:T(8,128)(4,1)}, u32[]{:S(2)}) copy-start(pred[8,17]{0,1:T(8,128)(4,1)} %constant.27) | copy-start | bytes 412
  196.3 17.1 %all-to-all-start.2 = ((f32[12,1,4614]{2,1,0:T(1,128)}), f32[12,1,4614]{2,1,0:T(1,128)S(1)}, u32[]{:S(2)}, u32[]{:S(2)}) async-start(f32[12,1,4614]{2,1,0:T(1,128)} %broadcast_in_dim.8), calls=%async_computation.2 | async-start | bytes 454656 | tf_op jit(solution)/shard_map/all_to_all | solution.py:33
where the time goes:
time: 240 us; the launch traced here: 235 us
  local copies, waits for them, and re-layouts  65.4 us (27%)
  waiting for transfers between devices  63.7 us (27%)
  starting transfers between devices  47.5 us (20%)
  matrix products  22.6 us (9%)
  blocking collectives  19.6 us (8%)
  other arithmetic  14.8 us (6%)
    ppermute x4, waiting for transfers between devices, extended(): after = lax.ppermute(initial, axis, down)  47.8 us
    ppermute x4, starting transfers between devices, extended(): before = lax.ppermute(last, axis, up)  26.5 us
    all_to_all x1, blocking collectives, sent_and_summed(): blocks = lax.all_to_all(in_blocks(shard, dim, size), axis, 0, 0, tiled=True)  19.6 us
    unnamed x24, local copies, waits for them, and re-layouts  19.2 us
    all_to_all x2, starting transfers between devices, sent_to_all(): return lax.all_to_all(copies, axis, split_axis=0, concat_axis=0, tiled=True)  15.8 us
    conv_general_dilated x1, matrix products, filter_terms(): lax.conv_general_dilated(padded, delta, (1, 1, 1), ((0, 0), (0, 0), (1, 1...  15.1 us
    conv_general_dilated x1, local copies, waits for them, and re-layouts, filter_terms(): lax.conv_general_dilated(padded, delta, (1, 1, 1), ((0, 0), (0, 0), (1, 1...  12.1 us
    concatenate x4, other arithmetic, extended(): shard = jnp.concatenate([before, shard, after], axis=dim)  11.9 us
  transfers between devices with their start and end apart: 10, of which 9 were waited for; matrix products, arithmetic and copies ran while one was open for 5% of the time, Pallas kernels for 0%

commit v1 on v0

v1 whole, which is shorter than its diff:
```python
import jax
import jax.numpy as jnp
from jax import lax
from jax.experimental import pallas as pl
from jax.experimental.pallas import tpu as pltpu
from jax.sharding import PartitionSpec as P

BF = jnp.bfloat16
F32 = jnp.float32
CI, CO, NX, NY, NZ = 32, 64, 2, 8, 128
GROUP = ("sx", "sy")
NT_DIMS = (((1,), (1,)), ((), ()))
VM = pl.BlockSpec(memory_space=pltpu.VMEM)
SM = pl.BlockSpec(memory_space=pltpu.SMEM)
ROWS = 480


def call(body, outs, scratch=(), n_in=1, smem=0, flops=0):
    return pl.pallas_call(
        body,
        out_shape=outs,
        in_specs=[SM] * smem + [VM] * (n_in - smem),
        out_specs=jax.tree.map(lambda _: VM, outs),
        scratch_shapes=list(scratch),
        cost_estimate=pl.CostEstimate(flops=flops, bytes_accessed=1 << 20, transcendentals=0),
    )


def turn_volume(sy_ref, v_ref, t_ref, edge_ref, buf):
    buf[...] = v_ref[...].astype(F32).reshape(CI * NX * NY, NZ)
    for x in range(NX):
        for y in range(NY):
            t_ref[x, y] = buf[pl.ds(x * NY + y, CI, stride=NX * NY), :].astype(BF)
    edge = (1 - sy_ref[0]) * (NY - 1)
    for x in range(NX):
        edge_ref[x] = buf[pl.ds(x * NY + edge, CI, stride=NX * NY), :].astype(BF)


def prepare(w_ref, u_ref, fwd_ref, bwd_ref, t_ref, buf):
    eye = (
        lax.broadcasted_iota(jnp.int32, (CO, CO), 0) == lax.broadcasted_iota(jnp.int32, (CO, CO), 1)
    ).astype(BF)
    for c in range(3):
        taps = jnp.concatenate(
            [w_ref[(ab * 3 + c) * CI : (ab * 3 + c + 1) * CI, :] for ab in range(9)], axis=0
        )
        fwd_ref[c * CO : (c + 1) * CO, :] = lax.dot_general(
            eye, taps, NT_DIMS, preferred_element_type=F32
        ).astype(BF)
        for ab in range(9):
            back = (2 - ab // 3) * 3 + 2 - ab % 3
            bwd_ref[c * CI : (c + 1) * CI, back * CO : (back + 1) * CO] = w_ref[
                (ab * 3 + c) * CI : (ab * 3 + c + 1) * CI, :
            ]
    buf[...] = u_ref[...].astype(F32).reshape(CO * NX * NY, NZ)
    for p in range(NX * NY):
        t_ref[p] = buf[pl.ds(p, CO, stride=NX * NY), :].astype(BF)


def fill(ext, sy, own, before, after, row, corner_lo, corner_hi):
    for x in range(NX):
        for y in range(NY):
            ext[x + 1, y + 1] = own[x, y]
    for y in range(NY):
        ext[0, y + 1] = before[y]
        ext[3, y + 1] = after[y]
    far = (1 - sy) * (NY + 1)
    near = sy * (NY + 1)
    nothing = jnp.zeros(ext.shape[2:], BF)
    for x in range(4):
        ext[x, near] = nothing
    ext[0, far] = corner_lo
    ext[1, far] = row[0]
    ext[2, far] = row[1]
    ext[3, far] = corner_hi


def window(ext, x, y, channels):
    parts = []
    for dy in range(2):
        parts.append(
            jnp.concatenate(
                [ext[x + a, y + dy : y + dy + 3].reshape(3 * channels, NZ) for a in range(3)], axis=0
            )
        )
    return parts


def moved(v, shift):
    lane = lax.broadcasted_iota(jnp.int32, v.shape, 1)
    if shift == 1:
        return jnp.where(lane == 0, 0.0, pltpu.roll(v, 1, 1))
    return jnp.where(lane == NZ - 1, 0.0, pltpu.roll(v, NZ - 1, 1))


def forward(
    sy_ref, t_ref, before_ref, after_ref, row_ref, lo_ref, hi_ref, fwd_ref, up_ref, bias_ref,
    act_ref, delta_ref, edge_ref, sum_ref, ext, acc,
):
    sy = sy_ref[0]
    fill(ext, sy, t_ref, before_ref, after_ref, row_ref, lo_ref[...], hi_ref[...])
    acc[...] = jnp.zeros_like(acc)
    ones = jnp.ones((16, 2 * NZ), BF)
    none = jnp.zeros((CO, 2 * NZ), BF)
    for x in range(NX):
        for y in range(0, NY, 2):
            first, second = window(ext, x, y, CI)
            cols = jnp.concatenate([first, second], axis=1)
            part = jnp.dot(fwd_ref[...], cols, preferred_element_type=F32)
            shifted = [[], [], []]
            for k in range(2):
                at = slice(k * NZ, (k + 1) * NZ)
                pre = (
                    moved(part[:CO, at], 1)
                    + part[CO : 2 * CO, at]
                    + moved(part[2 * CO :, at], -1)
                    + bias_ref[...]
                )
                e = jnp.exp(-jnp.abs(pre))
                r = 1.0 / (1.0 + e)
                sig = jnp.where(pre >= 0, r, e * r)
                soft = jnp.maximum(pre, 0.0) + jnp.log1p(e)
                p = x * NY + y + k
                act_ref[p] = (0.3 * pre + 0.7 * soft).astype(BF)
                d = (up_ref[p].astype(F32) * (0.3 + 0.7 * sig)).astype(BF)
                delta_ref[x, y + k] = d
                wide = d.astype(F32)
                shifted[0].append(moved(wide, -1).astype(BF))
                shifted[1].append(d)
                shifted[2].append(moved(wide, 1).astype(BF))
            right = jnp.concatenate(
                [jnp.concatenate(s, axis=1) for s in shifted] + [none], axis=0
            )
            left = jnp.concatenate([cols, ones], axis=0)
            acc[...] += lax.dot_general(left, right, NT_DIMS, preferred_element_type=F32)
    edge = (1 - sy) * (NY - 1)
    for x in range(NX):
        edge_ref[x] = delta_ref[x, edge]
    n = 9 * CI
    sum_ref[0:n, :] = acc[0:n, 0:NZ].astype(sum_ref.dtype)
    half = n // 2
    sum_ref[n : n + half, :] = (
        acc[0:half, NZ:] + pltpu.roll(acc[half:n, NZ:], CO, 1)
    ).astype(sum_ref.dtype)
    sum_ref[n + half : n + half + 8, :] = acc[n : n + 8, 0:NZ].astype(sum_ref.dtype)
    sum_ref[n + half + 8 :, :] = jnp.zeros((ROWS - n - half - 8, NZ), sum_ref.dtype)


def backward(
    sy_ref, d_ref, before_ref, after_ref, row_ref, lo_ref, hi_ref, bwd_ref, act_ref,
    out_ref, grad_ref, ext, wide, narrow,
):
    for p in range(NX * NY):
        wide[pl.ds(p, CO, stride=NX * NY), :] = act_ref[p].astype(F32)
    out_ref[...] = wide[...].reshape(CO, NX, NY, NZ).astype(BF)
    fill(ext, sy_ref[0], d_ref, before_ref, after_ref, row_ref, lo_ref[...], hi_ref[...])
    for x in range(NX):
        for y in range(0, NY, 2):
            first, second = window(ext, x, y, CO)
            cols = jnp.concatenate([first, second], axis=1)
            part = jnp.dot(bwd_ref[...], cols, preferred_element_type=F32)
            for k in range(2):
                at = slice(k * NZ, (k + 1) * NZ)
                g = (
                    moved(part[:CI, at], -1)
                    + part[CI : 2 * CI, at]
                    + moved(part[2 * CI :, at], 1)
                )
                narrow[pl.ds(x * NY + y + k, CI, stride=NX * NY), :] = g
    grad_ref[...] = narrow[...].reshape(CI, NX, NY, NZ).astype(BF)


def finish(norm_ref, s_ref, w_ref, b_ref):
    norm = norm_ref[0]
    n, half = 9 * CI, 9 * CI // 2
    total = s_ref[...].astype(F32) * norm
    for ab in range(9):
        at = ab * CI
        w_ref[(ab * 3) * CI : (ab * 3 + 1) * CI, :] = total[at : at + CI, :CO]
        w_ref[(ab * 3 + 1) * CI : (ab * 3 + 2) * CI, :] = pltpu.roll(
            total[at : at + CI, :], CO, 1
        )[:, :CO]
    last = jnp.concatenate(
        [total[n : n + half], pltpu.roll(total[n : n + half], CO, 1)], axis=0
    )[:, :CO]
    for ab in range(9):
        w_ref[(ab * 3 + 2) * CI : (ab * 3 + 3) * CI, :] = last[ab * CI : (ab + 1) * CI]
    b_ref[...] = pltpu.roll(total[n + half : n + half + 8, :], CO, 1)[:, :CO]


def everywhere(blocks, axis):
    return lax.all_to_all(blocks, axis, 0, 0, tiled=True)


def copies(share, axis):
    return everywhere(jnp.broadcast_to(share[None], (lax.axis_size(axis), *share.shape)), axis)


def reduced(part):
    groups = lax.axis_size(GROUP)
    send = part.reshape(groups, ROWS // groups, NZ)
    share = jnp.sum(everywhere(send, GROUP).astype(F32), axis=0).astype(part.dtype)
    share = jnp.sum(copies(share, "samp").astype(F32), axis=0).astype(part.dtype)
    return copies(share, GROUP).reshape(ROWS, NZ)


def neighbours(t, row):
    n = lax.axis_size("sx")
    up = [(i, i + 1) for i in range(n - 1)]
    down = [(j, i) for i, j in up]
    before = lax.ppermute(t[NX - 1], "sx", up)
    after = lax.ppermute(t[0], "sx", down)
    here = (1 - lax.axis_index("sy")) * (NY - 1)
    lo = lax.dynamic_index_in_dim(before, here, 0, keepdims=True)
    hi = lax.dynamic_index_in_dim(after, here, 0, keepdims=True)
    swapped = lax.ppermute(jnp.concatenate([lo, row, hi], axis=0), "sy", [(0, 1), (1, 0)])
    return before, after, swapped[1:3], swapped[0], swapped[3]


def per_device(volume, kernel, bias, upstream, dt=BF):
    s = jax.ShapeDtypeStruct
    sy = lax.axis_index("sy").astype(jnp.int32).reshape(1)
    taps = jnp.transpose(kernel, (2, 3, 4, 1, 0)).reshape(27 * CI, CO)
    t, row = call(
        turn_volume,
        (s((NX, NY, CI, NZ), BF), s((NX, CI, NZ), BF)),
        [pltpu.VMEM((CI * NX * NY, NZ), F32)], 2, 1, 10**8,
    )(sy, volume[0])
    fwd, bwd, up = call(
        prepare,
        (s((3 * CO, 9 * CI), BF), s((3 * CI, 9 * CO), BF), s((NX * NY, CO, NZ), BF)),
        [pltpu.VMEM((CO * NX * NY, NZ), F32)], 2, 0, 10**9,
    )(taps, upstream[0])
    bias_wide = jnp.broadcast_to(bias[:, None], (CO, NZ))
    act, delta, edge, part = call(
        forward,
        (s((NX * NY, CO, NZ), BF), s((NX, NY, CO, NZ), BF), s((NX, CO, NZ), BF), s((ROWS, NZ), dt)),
        [pltpu.VMEM((4, NY + 2, CI, NZ), BF), pltpu.VMEM((9 * CI + 16, 2 * NZ), F32)], 10, 1, 4 * 10**9,
    )(sy, t, *neighbours(t, row), fwd, up, bias_wide)
    summed = reduced(part)
    out, grad = call(
        backward,
        (s((CO, NX, NY, NZ), BF), s((CI, NX, NY, NZ), BF)),
        [
            pltpu.VMEM((4, NY + 2, CO, NZ), BF),
            pltpu.VMEM((CO * NX * NY, NZ), F32),
            pltpu.VMEM((CI * NX * NY, NZ), F32),
        ],
        9, 1, 4 * 10**9,
    )(sy, delta, *neighbours(delta, edge), bwd, act)
    whole = lax.axis_size("samp") * lax.axis_size(GROUP) * NX * NY * NZ
    norm = (1.0 / jnp.sqrt(jnp.float32(whole))).reshape(1)
    w, b = call(finish, (s((27 * CI, CO), F32), s((8, CO), F32)), (), 2, 1, 10**8)(norm, summed)
    wgrad = jnp.transpose(w.reshape(3, 3, 3, CI, CO), (4, 3, 0, 1, 2))
    return out[None], grad[None], wgrad, b[0]


def solution(mesh):
    spec = P("samp", None, "sx", "sy", None)
    return jax.shard_map(
        per_device, mesh=mesh, in_specs=(spec, P(), P(), spec), out_specs=(spec, spec, P(), P()), check_vma=False
    )
```

time: 240 us -> 116 us (0.48); the launches traced: 235 us -> 115 us
  local copies, waits for them, and re-layouts: 65.4 us -> 7.56 us
  waiting for transfers between devices: 63.7 us -> 21.4 us
  matrix products: 22.6 us -> 0 us
  other arithmetic: 14.8 us -> 0.16 us
  Pallas kernels: 0 us -> 12.5 us
  blocking collectives: 19.6 us -> 23.1 us
    ppermute x8 -> x6, waiting for transfers between devices: 56.9 us -> 13.5 us  [the longest x2 8.93 us: neighbours(): lax.ppermute(jnp.concatenate([lo, row, hi], axis=0), 'sy', [(0, 1), (1, 0)])]
    conv_general_dilated x3 -> x0, matrix products: 22.6 us -> none  [the longest x1 15.1 us: filter_terms(): lax.conv_general_dilated(padded, delta, (1, 1, 1), ((0, 0), (0, 0), (1, 1...]
    unnamed x24 -> x18, local copies, waits for them, and re-layouts: 19.2 us -> 0.73 us
    conv_general_dilated x5 -> x0, local copies, waits for them, and re-layouts: 12.6 us -> none  [the longest x1 12.1 us: filter_terms(): lax.conv_general_dilated(padded, delta, (1, 1, 1), ((0, 0), (0, 0), (1, 1...]
    pallas_call x0 -> x5, Pallas kernels: none -> 12.5 us  [the longest x1 4.05 us: per_device(): call(forward, (s((NX * NY, CO, NZ), BF), s((NX, NY, CO, NZ), BF), s((NX,...]
    concatenate x5 -> x2, other arithmetic: 12 us -> 0.02 us  [neighbours(): jnp.concatenate([lo, row, hi], axis=0)]
    reshape x2 -> x0, local copies, waits for them, and re-layouts: 10.5 us -> none  [the longest x1 10.4 us: per_device(): joined = jnp.concatenate([wgrad.reshape(-1), bgrad])]
    mul x1 -> x0, local copies, waits for them, and re-layouts: 8.33 us -> none  [per_device(): return (activated, input_grad, wsum * norm, bsum * norm)]
  transfers between devices with their start and end apart: 10 -> 8, of which waited for: 9 -> 6; matrix products, arithmetic and copies ran while one was open for 5% -> 1% of each run, Pallas kernels for 0% -> 4%
where the time goes in v1:
time: 116 us; the launch traced here: 115 us
  starting transfers between devices  49.4 us (43%)
  blocking collectives  23.1 us (20%)
  waiting for transfers between devices  21.4 us (18%)
  Pallas kernels  12.5 us (11%)
  local copies, waits for them, and re-layouts  7.56 us (7%)
    all_to_all x1, blocking collectives, everywhere(): return lax.all_to_all(blocks, axis, 0, 0, tiled=True)  23.1 us
    ppermute x2, starting transfers between devices, neighbours(): lax.ppermute(jnp.concatenate([lo, row, hi], axis=0), 'sy', [(0, 1), (1, 0)])  19.2 us
    all_to_all x2, starting transfers between devices, everywhere(): return lax.all_to_all(blocks, axis, 0, 0, tiled=True)  18.2 us
    ppermute x2, starting transfers between devices, neighbours(): before = lax.ppermute(t[NX - 1], 'sx', up)  9.46 us
    ppermute x2, waiting for transfers between devices, neighbours(): lax.ppermute(jnp.concatenate([lo, row, hi], axis=0), 'sy', [(0, 1), (1, 0)])  8.93 us
    all_to_all x2, waiting for transfers between devices, everywhere(): return lax.all_to_all(blocks, axis, 0, 0, tiled=True)  7.86 us
    pallas_call x1, Pallas kernels, per_device(): call(forward, (s((NX * NY, CO, NZ), BF), s((NX, NY, CO, NZ), BF), s((NX,...  4.05 us
    pallas_call x1, Pallas kernels, per_device(): call(backward, (s((CO, NX, NY, NZ), BF), s((CI, NX, NY, NZ), BF)), [pltpu...  2.91 us
  transfers between devices with their start and end apart: 8, of which 6 were waited for; matrix products, arithmetic and copies ran while one was open for 1% of the time, Pallas kernels for 4%

profile of v1, /device:TPU:2, one launch (start us, length us, event | category | flops | bytes accessed | tf_op | source)
XLA Modules:
  0.0 114.8 jit_solution(1155142185316681136)
XLA Ops:
  0.6 1.7 %shard_map.75 = (bf16[2,8,32,128]{3,2,1,0:T(8,128)(2,1)}, bf16[2,32,128]{2,1,0:T(8,128)(2,1)}) custom-call(s32[1]{0:T(128)} %bitcast.sy_ref, bf16[32,2,8,128]{3,2,1,0:T(8,128)(2,1)} %bitcast.35), custom_call_target="tpu_custom_call" | custom-call | flops 100000000 | bytes 1048576 | tf_op jit(solution)/shard_map/pallas_call | solution.py:224
  2.3 0.9 slice_bitcast_fusion.2
  3.2 1.3 %collective-permute-start.1 = (bf16[8,32,128]{2,1,0:T(8,128)(2,1)S(1)}, bf16[8,32,128]{2,1,0:T(8,128)(2,1)S(1)}, u32[]{:S(2)}, u32[]{:S(2)}) collective-permute-start(bf16[8,32,128]{2,1,0:T(8,128)(2,1)S(1)} %get-tuple-element.32), channel_id=1, source_target_pairs={{2,0},{4,2},{6,4},{8,6},{10,8},{3,1},{5,3},{7,5},{9,7},{11,9},{14,... | collective-permute-start | bytes 196616 | tf_op jit(solution)/shard_map/ppermute | solution.py:212
  4.5 4.9 %collective-permute-start = (bf16[8,32,128]{2,1,0:T(8,128)(2,1)S(1)}, bf16[8,32,128]{2,1,0:T(8,128)(2,1)S(1)}, u32[]{:S(2)}, u32[]{:S(2)}) collective-permute-start(bf16[8,32,128]{2,1,0:T(8,128)(2,1)S(1)} %get-tuple-element.33), channel_id=1, source_target_pairs={{0,2},{2,4},{4,6},{6,8},{8,10},{1,3},{3,5},{5,7},{7,9},{9,11},{12,... | collective-permute-start | bytes 196616 | tf_op jit(solution)/shard_map/ppermute | solution.py:211
  9.4 0.0 copy-start.3
  9.4 0.3 collective-permute-done.1.after_ref
  9.7 0.0 copy-start.6
  9.7 1.6 %collective-permute-done.before_ref = bf16[8,32,128]{2,1,0:T(8,128)(2,1)S(1)} collective-permute-done((bf16[8,32,128]{2,1,0:T(8,128)(2,1)S(1)}, bf16[8,32,128]{2,1,0:T(8,128)(2,1)S(1)}, u32[]{:S(2)}, u32[]{:S(2)}) %collective-permute-start) | collective-permute-done | bytes 65568 | tf_op jit(solution)/shard_map/ppermute | solution.py:211
  11.3 0.0 copy-start.7
  11.3 0.0 copy-done.3
  11.3 14.8 %collective-permute-start.2 = (bf16[4,32,128]{2,1,0:T(8,128)(2,1)S(1)}, bf16[4,32,128]{2,1,0:T(8,128)(2,1)S(1)}, u32[]{:S(2)}, u32[]{:S(2)}) collective-permute-start(bf16[4,32,128]{2,1,0:T(8,128)(2,1)S(1)} %pad_maximum_fusion.1), channel_id=1, source_target_pairs={{0,1},{1,0},{2,3},{3,2},{4,5},{5,4},{6,7},{7,6},{8,9},{9,8},{10,11... | collective-permute-start | bytes 98312 | tf_op jit(solution)/shard_map/ppermute | solution.py:216
  26.1 2.1 %shard_map.76 = (bf16[192,288]{1,0:T(8,128)(2,1)}, bf16[96,576]{1,0:T(8,128)(2,1)}, bf16[16,64,128]{2,1,0:T(8,128)(2,1)}) custom-call(bf16[864,64]{1,0:T(8,128)(2,1)} %bitcast.34, bf16[64,2,8,128]{3,2,1,0:T(8,128)(2,1)} %bitcast.33), custom_call_target="tpu_custom_call" | custom-call | flops 1000000000 | bytes 1048576 | tf_op jit(solution)/shard_map/pallas_call | solution.py:229
  28.2 0.0 copy-done.6
  28.2 0.0 copy-done.7
  28.3 0.0 collective-permute-done.2
  28.3 0.6 slice.44.row_ref
  28.9 0.0 copy-start.8
  28.9 0.6 slice_bitcast_fusion.6
  29.5 0.1 copy-done.8
  29.5 0.7 broadcast_in_dim.10.bias_ref
  30.2 4.0 %shard_map.77 = (bf16[16,64,128]{2,1,0:T(8,128)(2,1)}, bf16[2,8,64,128]{3,2,1,0:T(8,128)(2,1)}, bf16[2,64,128]{2,1,0:T(8,128)(2,1)}, bf16[480,128]{1,0:T(8,128)(2,1)}) custom-call(s32[1]{0:T(128)} %bitcast.sy_ref, bf16[2,8,32,128]{3,2,1,0:T(8,128)(2,1)} %get-tuple-element.17.t_ref, bf16[8,32,128]{2,1,0:T(8,128)(2,1)} %copy-done.7, ...), custom_call_target="tpu_custom_call" | custom-call | flops 4000000000 | bytes 1048576 | tf_op jit(solution)/shard_map/pallas_call | solution.py:235
  34.3 23.1 %all_to_all.15 = bf16[12,40,128]{2,1,0:T(8,128)(2,1)S(1)} all-to-all(bf16[12,40,128]{2,1,0:T(8,128)(2,1)} %bitcast.32), channel_id=1, replica_groups=mesh['samp'=64,'sx'=6,'sy'=2] {'sx','sy'}, dimensions={0} | all-to-all | bytes 245760 | tf_op jit(solution)/shard_map/all_to_all | solution.py:192
  57.3 1.0 broadcast_in_dim.13
  58.3 0.0 copy-start
  58.3 10.8 %all-to-all-start.1 = ((bf16[64,40,128]{2,1,0:T(8,128)(2,1)}), bf16[64,40,128]{2,1,0:T(8,128)(2,1)S(1)}, u32[]{:S(2)}, u32[]{:S(2)}) async-start(bf16[64,40,128]{2,1,0:T(8,128)(2,1)} %broadcast_in_dim.13), calls=%async_computation.1 | async-start | bytes 1310720 | tf_op jit(solution)/shard_map/all_to_all | solution.py:192
  69.1 0.0 copy-done
  69.1 1.3 %collective-permute-start.4 = (bf16[8,64,128]{2,1,0:T(8,128)(2,1)S(1)}, bf16[8,64,128]{2,1,0:T(8,128)(2,1)S(1)}, u32[]{:S(2)}, u32[]{:S(2)}) collective-permute-start(bf16[8,64,128]{2,1,0:T(8,128)(2,1)S(1)} %get-tuple-element.30), channel_id=1, source_target_pairs={{2,0},{4,2},{6,4},{8,6},{10,8},{3,1},{5,3},{7,5},{9,7},{11,9},{14,... | collective-permute-start | bytes 393224 | tf_op jit(solution)/shard_map/ppermute | solution.py:212
  70.4 0.0 copy-start.2
  70.4 4.6 %collective-permute-start.3 = (bf16[8,64,128]{2,1,0:T(8,128)(2,1)S(1)}, bf16[8,64,128]{2,1,0:T(8,128)(2,1)S(1)}, u32[]{:S(2)}, u32[]{:S(2)}) collective-permute-start(bf16[8,64,128]{2,1,0:T(8,128)(2,1)S(1)} %get-tuple-element.31), channel_id=1, source_target_pairs={{0,2},{2,4},{4,6},{6,8},{8,10},{1,3},{3,5},{5,7},{7,9},{9,11},{12,... | collective-permute-start | bytes 393224 | tf_op jit(solution)/shard_map/ppermute | solution.py:211
  75.0 1.5 %collective-permute-done.4.after_ref = bf16[8,64,128]{2,1,0:T(8,128)(2,1)S(1)} collective-permute-done((bf16[8,64,128]{2,1,0:T(8,128)(2,1)S(1)}, bf16[8,64,128]{2,1,0:T(8,128)(2,1)S(1)}, u32[]{:S(2)}, u32[]{:S(2)}) %collective-permute-start.4) | collective-permute-done | bytes 131104 | tf_op jit(solution)/shard_map/ppermute | solution.py:212
  76.5 0.0 copy-start.4
  76.5 1.2 %collective-permute-done.3.before_ref = bf16[8,64,128]{2,1,0:T(8,128)(2,1)S(1)} collective-permute-done((bf16[8,64,128]{2,1,0:T(8,128)(2,1)S(1)}, bf16[8,64,128]{2,1,0:T(8,128)(2,1)S(1)}, u32[]{:S(2)}, u32[]{:S(2)}) %collective-permute-start.3) | collective-permute-done | bytes 131104 | tf_op jit(solution)/shard_map/ppermute | solution.py:211
  77.7 0.0 copy-start.5
  77.7 0.0 copy-done.2
  77.8 4.3 %collective-permute-start.5 = (bf16[4,64,128]{2,1,0:T(8,128)(2,1)S(1)}, bf16[4,64,128]{2,1,0:T(8,128)(2,1)S(1)}, u32[]{:S(2)}, u32[]{:S(2)}) collective-permute-start(bf16[4,64,128]{2,1,0:T(8,128)(2,1)S(1)} %pad_maximum_fusion), channel_id=1, source_target_pairs={{0,1},{1,0},{2,3},{3,2},{4,5},{5,4},{6,7},{7,6},{8,9},{9,8},{10,11... | collective-permute-start | bytes 196616 | tf_op jit(solution)/shard_map/ppermute | solution.py:216
  82.1 8.9 %collective-permute-done.5 = bf16[4,64,128]{2,1,0:T(8,128)(2,1)S(1)} collective-permute-done((bf16[4,64,128]{2,1,0:T(8,128)(2,1)S(1)}, bf16[4,64,128]{2,1,0:T(8,128)(2,1)S(1)}, u32[]{:S(2)}, u32[]{:S(2)}) %collective-permute-start.5) | collective-permute-done | bytes 65568 | tf_op jit(solution)/shard_map/ppermute | solution.py:216
  91.0 0.6 slice.47.row_ref
  91.6 0.0 copy-done.4
  91.6 0.6 slice_bitcast_fusion.4
  92.3 0.0 copy-done.5
  92.3 0.0 all-to-all-done.1
  92.3 0.1 reduce_sum.25
  92.4 0.7 broadcast_in_dim.28
  93.0 7.4 %all-to-all-start.2 = ((bf16[12,40,128]{2,1,0:T(8,128)(2,1)}), bf16[12,40,128]{2,1,0:T(8,128)(2,1)S(1)}, u32[]{:S(2)}, u32[]{:S(2)}) async-start(bf16[12,40,128]{2,1,0:T(8,128)(2,1)} %broadcast_in_dim.28), calls=%async_computation.2 | async-start | bytes 245760 | tf_op jit(solution)/shard_map/all_to_all | solution.py:192
  100.5 2.9 %shard_map.78 = (bf16[64,2,8,128]{3,2,1,0:T(8,128)(2,1)}, bf16[32,2,8,128]{3,2,1,0:T(8,128)(2,1)}) custom-call(s32[1]{0:T(128)} %bitcast.sy_ref, bf16[2,8,64,128]{3,2,1,0:T(8,128)(2,1)} %get-tuple-element.21.d_ref, bf16[8,64,128]{2,1,0:T(8,128)(2,1)} %copy-done.5, bf16[8,64,128]{2,1,0:T(8,128)(2,1)} %copy-done.4, bf16[2,64,128]{2,1,0:T(8,128)(2,1)} %slice.47.row_ref, ...), custom_call_target="tpu_custom_call" | custom-call | flops 4000000000 | bytes 1048576 | tf_op jit(solution)/shard_map/pallas_call | solution.py:241
  103.4 7.9 %all-to-all-done.2 = bf16[12,40,128]{2,1,0:T(8,128)(2,1)S(1)} async-done(((bf16[12,40,128]{2,1,0:T(8,128)(2,1)}), bf16[12,40,128]{2,1,0:T(8,128)(2,1)S(1)}, u32[]{:S(2)}, u32[]{:S(2)}) %all-to-all-start.2) | async-done | bytes 122912 | tf_op jit(solution)/shard_map/all_to_all | solution.py:192
  111.2 0.0 copy-start.1
  111.2 0.6 copy-done.1
  111.9 1.8 %shard_map.79 = (f32[864,64]{1,0:T(8,128)}, f32[8,64]{1,0:T(8,128)}) custom-call(f32[1]{0:T(128)} %constant.26.clone.1.norm_ref, bf16[480,128]{1,0:T(8,128)(2,1)} %bitcast.31), custom_call_target="tpu_custom_call" | custom-call | flops 100000000 | bytes 1048576 | tf_op jit(solution)/shard_map/pallas_call | solution.py:253
  113.7 1.2 %slice_bitcast_fusion.8 = f32[64]{0:T(128)} fusion(f32[8,64]{1,0:T(8,128)} %get-tuple-element.29), kind=kLoop, calls=%fused_computation.14 | loop fusion | bytes 512 | tf_op jit(solution)/shard_map/squeeze | solution.py:255
  (8 shorter events, 0.1 us)
Async XLA Ops:
  3.2 6.5 %collective-permute-start.1 = (bf16[8,32,128]{2,1,0:T(8,128)(2,1)S(1)}, bf16[8,32,128]{2,1,0:T(8,128)(2,1)S(1)}, u32[]{:S(2)}, u32[]{:S(2)}) collective-permute-start(bf16[8,32,128]{2,1,0:T(8,128)(2,1)S(1)} %get-tuple-element.32), channel_id=1, source_target_pairs={{2,0},{4,2},{6,4},{8,6},{10,8},{3,1},{5,3},{7,5},{9,7},{11,9},{14,... | collective-permute-start | bytes 196616 | tf_op jit(solution)/shard_map/ppermute | solution.py:212
  4.5 6.8 %collective-permute-start = (bf16[8,32,128]{2,1,0:T(8,128)(2,1)S(1)}, bf16[8,32,128]{2,1,0:T(8,128)(2,1)S(1)}, u32[]{:S(2)}, u32[]{:S(2)}) collective-permute-start(bf16[8,32,128]{2,1,0:T(8,128)(2,1)S(1)} %get-tuple-element.33), channel_id=1, source_target_pairs={{0,2},{2,4},{4,6},{6,8},{8,10},{1,3},{3,5},{5,7},{7,9},{9,11},{12,... | collective-permute-start | bytes 196616 | tf_op jit(solution)/shard_map/ppermute | solution.py:211
  9.4 1.9 %copy-start.3 = (bf16[2,32,128]{2,1,0:T(8,128)(2,1)S(1)}, bf16[2,32,128]{2,1,0:T(8,128)(2,1)}, u32[]{:S(2)}) copy-start(bf16[2,32,128]{2,1,0:T(8,128)(2,1)} %get-tuple-element.18) | copy-start | bytes 49156
  9.7 18.6 %copy-start.6 = (bf16[8,32,128]{2,1,0:T(8,128)(2,1)}, bf16[8,32,128]{2,1,0:T(8,128)(2,1)S(1)}, u32[]{:S(2)}) copy-start(bf16[8,32,128]{2,1,0:T(8,128)(2,1)S(1)} %collective-permute-done.1.after_ref) | copy-start | bytes 196612
  11.3 17.0 %copy-start.7 = (bf16[8,32,128]{2,1,0:T(8,128)(2,1)}, bf16[8,32,128]{2,1,0:T(8,128)(2,1)S(1)}, u32[]{:S(2)}) copy-start(bf16[8,32,128]{2,1,0:T(8,128)(2,1)S(1)} %collective-permute-done.before_ref) | copy-start | bytes 196612
  11.3 17.0 %collective-permute-start.2 = (bf16[4,32,128]{2,1,0:T(8,128)(2,1)S(1)}, bf16[4,32,128]{2,1,0:T(8,128)(2,1)S(1)}, u32[]{:S(2)}, u32[]{:S(2)}) collective-permute-start(bf16[4,32,128]{2,1,0:T(8,128)(2,1)S(1)} %pad_maximum_fusion.1), channel_id=1, source_target_pairs={{0,1},{1,0},{2,3},{3,2},{4,5},{5,4},{6,7},{7,6},{8,9},{9,8},{10,11... | collective-permute-start | bytes 98312 | tf_op jit(solution)/shard_map/ppermute | solution.py:216
  28.9 0.7 copy-start.8
  58.3 10.8 %copy-start = (bf16[2,8,64,128]{3,2,1,0:T(8,128)(2,1)S(1)}, bf16[2,8,64,128]{3,2,1,0:T(8,128)(2,1)}, u32[]{:S(2)}) copy-start(bf16[2,8,64,128]{3,2,1,0:T(8,128)(2,1)} %get-tuple-element.21.d_ref) | copy-start | bytes 786436
  58.3 34.0 %all-to-all-start.1 = ((bf16[64,40,128]{2,1,0:T(8,128)(2,1)}), bf16[64,40,128]{2,1,0:T(8,128)(2,1)S(1)}, u32[]{:S(2)}, u32[]{:S(2)}) async-start(bf16[64,40,128]{2,1,0:T(8,128)(2,1)} %broadcast_in_dim.13), calls=%async_computation.1 | async-start | bytes 1310720 | tf_op jit(solution)/shard_map/all_to_all | solution.py:192
  69.1 7.4 %collective-permute-start.4 = (bf16[8,64,128]{2,1,0:T(8,128)(2,1)S(1)}, bf16[8,64,128]{2,1,0:T(8,128)(2,1)S(1)}, u32[]{:S(2)}, u32[]{:S(2)}) collective-permute-start(bf16[8,64,128]{2,1,0:T(8,128)(2,1)S(1)} %get-tuple-element.30), channel_id=1, source_target_pairs={{2,0},{4,2},{6,4},{8,6},{10,8},{3,1},{5,3},{7,5},{9,7},{11,9},{14,... | collective-permute-start | bytes 393224 | tf_op jit(solution)/shard_map/ppermute | solution.py:212
  70.4 7.3 %copy-start.2 = (bf16[2,64,128]{2,1,0:T(8,128)(2,1)S(1)}, bf16[2,64,128]{2,1,0:T(8,128)(2,1)}, u32[]{:S(2)}) copy-start(bf16[2,64,128]{2,1,0:T(8,128)(2,1)} %get-tuple-element.22) | copy-start | bytes 98308
  70.4 7.3 %collective-permute-start.3 = (bf16[8,64,128]{2,1,0:T(8,128)(2,1)S(1)}, bf16[8,64,128]{2,1,0:T(8,128)(2,1)S(1)}, u32[]{:S(2)}, u32[]{:S(2)}) collective-permute-start(bf16[8,64,128]{2,1,0:T(8,128)(2,1)S(1)} %get-tuple-element.31), channel_id=1, source_target_pairs={{0,2},{2,4},{4,6},{6,8},{8,10},{1,3},{3,5},{5,7},{7,9},{9,11},{12,... | collective-permute-start | bytes 393224 | tf_op jit(solution)/shard_map/ppermute | solution.py:211
  76.5 15.1 %copy-start.4 = (bf16[8,64,128]{2,1,0:T(8,128)(2,1)}, bf16[8,64,128]{2,1,0:T(8,128)(2,1)S(1)}, u32[]{:S(2)}) copy-start(bf16[8,64,128]{2,1,0:T(8,128)(2,1)S(1)} %collective-permute-done.4.after_ref) | copy-start | bytes 393220
  77.7 14.5 %copy-start.5 = (bf16[8,64,128]{2,1,0:T(8,128)(2,1)}, bf16[8,64,128]{2,1,0:T(8,128)(2,1)S(1)}, u32[]{:S(2)}) copy-start(bf16[8,64,128]{2,1,0:T(8,128)(2,1)S(1)} %collective-permute-done.3.before_ref) | copy-start | bytes 393220
  77.8 13.3 %collective-permute-start.5 = (bf16[4,64,128]{2,1,0:T(8,128)(2,1)S(1)}, bf16[4,64,128]{2,1,0:T(8,128)(2,1)S(1)}, u32[]{:S(2)}, u32[]{:S(2)}) collective-permute-start(bf16[4,64,128]{2,1,0:T(8,128)(2,1)S(1)} %pad_maximum_fusion), channel_id=1, source_target_pairs={{0,1},{1,0},{2,3},{3,2},{4,5},{5,4},{6,7},{7,6},{8,9},{9,8},{10,11... | collective-permute-start | bytes 196616 | tf_op jit(solution)/shard_map/ppermute | solution.py:216
  93.0 18.2 %all-to-all-start.2 = ((bf16[12,40,128]{2,1,0:T(8,128)(2,1)}), bf16[12,40,128]{2,1,0:T(8,128)(2,1)S(1)}, u32[]{:S(2)}, u32[]{:S(2)}) async-start(bf16[12,40,128]{2,1,0:T(8,128)(2,1)} %broadcast_in_dim.28), calls=%async_computation.2 | async-start | bytes 245760 | tf_op jit(solution)/shard_map/all_to_all | solution.py:192
  111.2 0.6 copy-start.1

commit v2 on v1

v2 whole, which is shorter than its diff:
```python
import jax
import jax.numpy as jnp
from jax import lax
from jax.experimental import pallas as pl
from jax.experimental.pallas import tpu as pltpu
from jax.sharding import Mesh
from jax.sharding import PartitionSpec as P


BF = jnp.bfloat16
F32 = jnp.float32
CI, CO, NX, NY, NZ = 32, 64, 2, 8, 128
GROUP = ("core", "sx", "sy")
SAMP = ("plane", "core")
NT_DIMS = (((1,), (1,)), ((), ()))
VM = pl.BlockSpec(memory_space=pltpu.VMEM)
SM = pl.BlockSpec(memory_space=pltpu.SMEM)
ROWS = 512


def call(body, outs, scratch=(), n_in=1, smem=0, flops=0):
    inner = pl.pallas_call(
        body,
        out_shape=outs,
        in_specs=[SM] * smem + [VM] * (n_in - smem),
        out_specs=jax.tree.map(lambda _: VM, outs),
        scratch_shapes=list(scratch),
        cost_estimate=pl.CostEstimate(flops=flops, bytes_accessed=1 << 20, transcendentals=0),
    )

    def run(*args):
        near = [pltpu.with_memory_space_constraint(a, pltpu.VMEM) for a in args[smem:]]
        return inner(*args[:smem], *near)

    return run


def turn_volume(sy_ref, v_ref, lo_ref, hi_ref, edge_ref, buf):
    buf[...] = v_ref[...].astype(F32).reshape(CI * NX * NY, NZ)
    for x, t_ref in enumerate((lo_ref, hi_ref)):
        for y in range(NY):
            t_ref[y] = buf[pl.ds(x * NY + y, CI, stride=NX * NY), :].astype(BF)
    edge = (1 - sy_ref[0]) * (NY - 1)
    for x in range(NX):
        edge_ref[x] = buf[pl.ds(x * NY + edge, CI, stride=NX * NY), :].astype(BF)


def prepare(w_ref, b_ref, u_ref, fwd_ref, bwd_ref, t_ref, wide_ref, buf):
    eye = lax.broadcasted_iota(jnp.int32, (CO, CO), 0) == lax.broadcasted_iota(jnp.int32, (CO, CO), 1)
    column = jnp.sum(jnp.where(eye, b_ref[...], 0.0), axis=1, keepdims=True)
    wide_ref[...] = jnp.broadcast_to(column, (CO, NZ))
    eye = eye.astype(BF)
    for c in range(3):
        taps = jnp.concatenate(
            [w_ref[(ab * 3 + c) * CI : (ab * 3 + c + 1) * CI, :] for ab in range(9)], axis=0
        )
        fwd_ref[c * CO : (c + 1) * CO, :] = lax.dot_general(
            eye, taps, NT_DIMS, preferred_element_type=F32
        ).astype(BF)
        for ab in range(9):
            back = (2 - ab // 3) * 3 + 2 - ab % 3
            bwd_ref[c * CI : (c + 1) * CI, back * CO : (back + 1) * CO] = w_ref[
                (ab * 3 + c) * CI : (ab * 3 + c + 1) * CI, :
            ]
    buf[...] = u_ref[...].astype(F32).reshape(CO * NX * NY, NZ)
    for p in range(NX * NY):
        t_ref[p] = buf[pl.ds(p, CO, stride=NX * NY), :].astype(BF)


def fill(ext, sy, planes, rows):
    for x, plane in enumerate(planes):
        for y in range(NY):
            ext[x, y + 1] = plane[y]
    far = (1 - sy) * (NY + 1)
    near = sy * (NY + 1)
    nothing = jnp.zeros(ext.shape[2:], BF)
    for x in range(4):
        ext[x, near] = nothing
        ext[x, far] = rows[x]


def window(ext, x, y, channels):
    parts = []
    for dy in range(2):
        parts.append(
            jnp.concatenate(
                [ext[x + a, pl.ds(y + dy, 3)].reshape(3 * channels, NZ) for a in range(3)], axis=0
            )
        )
    return parts


def moved(v, shift):
    lane = lax.broadcasted_iota(jnp.int32, v.shape, 1)
    if shift == 1:
        return jnp.where(lane == 0, 0.0, pltpu.roll(v, 1, 1))
    return jnp.where(lane == NZ - 1, 0.0, pltpu.roll(v, NZ - 1, 1))


def two_rows(ext, x, y, at_y, fwd_ref, up_ref, bias_ref, act_ref, delta_refs):
    ones = jnp.ones((16, 2 * NZ), BF)
    none = jnp.zeros((CO, 2 * NZ), BF)
    first, second = window(ext, x, y, CI)
    cols = jnp.concatenate([first, second], axis=1)
    part = jnp.dot(fwd_ref[...], cols, preferred_element_type=F32)
    shifted = [[], [], []]
    for k in range(2):
        at = slice(k * NZ, (k + 1) * NZ)
        pre = (
            moved(part[:CO, at], 1)
            + part[CO : 2 * CO, at]
            + moved(part[2 * CO :, at], -1)
            + bias_ref[...]
        )
        e = jnp.exp(-jnp.abs(pre))
        r = 1.0 / (1.0 + e)
        sig = jnp.where(pre >= 0, r, e * r)
        soft = jnp.maximum(pre, 0.0) + jnp.log1p(e)
        p = x * NY + at_y + k
        act_ref[p] = (0.3 * pre + 0.7 * soft).astype(BF)
        d = (up_ref[p].astype(F32) * (0.3 + 0.7 * sig)).astype(BF)
        delta_refs[x][at_y + k] = d
        wide = d.astype(F32)
        shifted[0].append(moved(wide, -1).astype(BF))
        shifted[1].append(d)
        shifted[2].append(moved(wide, 1).astype(BF))
    right = jnp.concatenate([jnp.concatenate(s, axis=1) for s in shifted] + [none], axis=0)
    left = jnp.concatenate([cols, ones], axis=0)
    return lax.dot_general(left, right, NT_DIMS, preferred_element_type=F32)


def forward_near(
    sy_ref, before_ref, lo_ref, hi_ref, after_ref, fwd_ref, up_ref, bias_ref,
    act_ref, dlo_ref, dhi_ref, acc, ext,
):
    sy = sy_ref[0]
    for x, plane in enumerate((before_ref, lo_ref, hi_ref, after_ref)):
        for y in range(NY):
            ext[x, y + 1] = plane[y]
        ext[x, sy * (NY + 1)] = jnp.zeros(ext.shape[2:], BF)
        ext[x, (1 - sy) * (NY + 1)] = jnp.zeros(ext.shape[2:], BF)
    for x in range(NX):
        for j in range(NY // 2 - 1):
            y = 2 * j + 2 * sy
            part = two_rows(ext, x, y, y, fwd_ref, up_ref, bias_ref, act_ref, (dlo_ref, dhi_ref))
            if x + j:
                acc[...] += part
            else:
                acc[...] = part
        far = (1 - sy) * (NY - 2)
        for k in range(2):
            act_ref[x * NY + far + k] = jnp.zeros((CO, NZ), BF)
            (dlo_ref, dhi_ref)[x][far + k] = jnp.zeros((CO, NZ), BF)


def forward_far(
    sy_ref, before_ref, lo_ref, hi_ref, after_ref, row_ref, fwd_ref, up_ref, bias_ref,
    act_in, dlo_in, dhi_in, acc_in, act_ref, dlo_ref, dhi_ref, edge_ref, sum_ref, ext, acc,
):
    sy = sy_ref[0]
    act_ref[...] = act_in[...]
    dlo_ref[...] = dlo_in[...]
    dhi_ref[...] = dhi_in[...]
    rows = row_ref
    for x, plane in enumerate((before_ref, lo_ref, hi_ref, after_ref)):
        for y in range(3):
            ext[x, sy + y] = plane[(1 - sy) * (NY - 3) + y]
        ext[x, 3 * (1 - sy)] = rows[x]
    far = (1 - sy) * (NY - 2)
    acc[...] = acc_in[...]
    for x in range(NX):
        acc[...] += two_rows(ext, x, 0, far, fwd_ref, up_ref, bias_ref, act_ref, (dlo_ref, dhi_ref))
    edge = (1 - sy) * (NY - 1)
    edge_ref[0] = dlo_ref[edge]
    edge_ref[1] = dhi_ref[edge]
    n = 9 * CI
    sum_ref[0:n, :] = acc[0:n, 0:NZ].astype(sum_ref.dtype)
    half = n // 2
    sum_ref[n : n + half, :] = (
        acc[0:half, NZ:] + pltpu.roll(acc[half:n, NZ:], CO, 1)
    ).astype(sum_ref.dtype)
    sum_ref[n + half : n + half + 8, :] = acc[n : n + 8, 0:NZ].astype(sum_ref.dtype)
    sum_ref[n + half + 8 :, :] = jnp.zeros((ROWS - n - half - 8, NZ), sum_ref.dtype)


def backward(
    sy_ref, before_ref, lo_ref, hi_ref, after_ref, row_ref, bwd_ref, act_ref,
    out_ref, grad_ref, ext, wide, narrow,
):
    for p in range(NX * NY):
        wide[pl.ds(p, CO, stride=NX * NY), :] = act_ref[p].astype(F32)
    out_ref[...] = wide[...].reshape(CO, NX, NY, NZ).astype(BF)
    fill(ext, sy_ref[0], (before_ref, lo_ref, hi_ref, after_ref), row_ref)
    for x in range(NX):
        for y in range(0, NY, 2):
            first, second = window(ext, x, y, CO)
            cols = jnp.concatenate([first, second], axis=1)
            part = jnp.dot(bwd_ref[...], cols, preferred_element_type=F32)
            for k in range(2):
                at = slice(k * NZ, (k + 1) * NZ)
                g = (
                    moved(part[:CI, at], -1)
                    + part[CI : 2 * CI, at]
                    + moved(part[2 * CI :, at], 1)
                )
                narrow[pl.ds(x * NY + y + k, CI, stride=NX * NY), :] = g
    grad_ref[...] = narrow[...].reshape(CI, NX, NY, NZ).astype(BF)


def finish(norm_ref, s_ref, w_ref, b_ref):
    norm = norm_ref[0]
    n, half = 9 * CI, 9 * CI // 2
    total = s_ref[...].astype(F32) * norm
    for ab in range(9):
        at = ab * CI
        w_ref[(ab * 3) * CI : (ab * 3 + 1) * CI, :] = total[at : at + CI, :CO]
        w_ref[(ab * 3 + 1) * CI : (ab * 3 + 2) * CI, :] = pltpu.roll(
            total[at : at + CI, :], CO, 1
        )[:, :CO]
    last = jnp.concatenate(
        [total[n : n + half], pltpu.roll(total[n : n + half], CO, 1)], axis=0
    )[:, :CO]
    for ab in range(9):
        w_ref[(ab * 3 + 2) * CI : (ab * 3 + 3) * CI, :] = last[ab * CI : (ab + 1) * CI]
    b_ref[...] = pltpu.roll(total[n + half : n + half + 8, :], CO, 1)[0:1, :CO]


def everywhere(blocks, axis):
    return lax.all_to_all(blocks, axis, 0, 0, tiled=True)


def copies(share, axis):
    return everywhere(jnp.broadcast_to(share[None], (lax.axis_size(axis), *share.shape)), axis)


def total(blocks):
    return jnp.sum(blocks.astype(F32), axis=0).astype(blocks.dtype)


def reduced(part):
    shares = lax.axis_size("plane")
    share = everywhere(part.reshape(shares, ROWS // shares, NZ), "plane")
    share = total(share)
    share = copies(share, GROUP)
    share = total(share)
    share = copies(share, "plane")
    return share.reshape(ROWS, NZ)


def neighbours(first, last, row):
    n = lax.axis_size("sx")
    up = [(i, i + 1) for i in range(n - 1)]
    down = [(j, i) for i, j in up]
    before = lax.ppermute(last, "sx", up)
    after = lax.ppermute(first, "sx", down)
    here = (1 - lax.axis_index("sy")) * (NY - 1)
    lo = lax.dynamic_index_in_dim(before, here, 0, keepdims=True)
    hi = lax.dynamic_index_in_dim(after, here, 0, keepdims=True)
    swapped = lax.ppermute(jnp.concatenate([lo, row, hi], axis=0), "sy", [(0, 1), (1, 0)])
    return before, first, last, after, swapped


def per_device(volume, kernel, bias, upstream, dt=BF):
    s = pltpu.VMEM
    sy = lax.axis_index("sy").astype(jnp.int32).reshape(1)
    taps = jnp.transpose(kernel, (2, 3, 4, 1, 0)).reshape(27 * CI, CO)
    first, last, row = call(
        turn_volume,
        (s((NY, CI, NZ), BF), s((NY, CI, NZ), BF), s((NX, CI, NZ), BF)),
        [pltpu.VMEM((CI * NX * NY, NZ), F32)], 2, 1, 10**8,
    )(sy, volume[0])
    fwd, bwd, up, bias_wide = call(
        prepare,
        (s((3 * CO, 9 * CI), BF), s((3 * CI, 9 * CO), BF), s((NX * NY, CO, NZ), BF), s((CO, NZ), F32)),
        [pltpu.VMEM((CO * NX * NY, NZ), F32)], 3, 0, 10**9,
    )(taps, bias.reshape(1, CO), upstream[0])
    around = list(neighbours(first, last, row))
    shapes = (s((NX * NY, CO, NZ), BF), s((NY, CO, NZ), BF), s((NY, CO, NZ), BF))
    sums = (9 * CI + 16, 2 * NZ)
    early = call(
        forward_near, (*shapes, s(sums, F32)),
        [pltpu.VMEM((4, NY + 2, CI, NZ), BF)], 8, 1, 3 * 10**9,
    )(sy, *around[:4], fwd, up, bias_wide)
    act, dfirst, dlast, edge, part = call(
        forward_far, (*shapes, s((NX, CO, NZ), BF), s((ROWS, NZ), dt)),
        [pltpu.VMEM((4, 4, CI, NZ), BF), pltpu.VMEM(sums, F32)], 13, 1, 10**9,
    )(sy, *around, fwd, up, bias_wide, *early)
    summed = reduced(part)
    o = jax.ShapeDtypeStruct
    out, grad = call(
        backward,
        (o((CO, NX, NY, NZ), BF), o((CI, NX, NY, NZ), BF)),
        [
            pltpu.VMEM((4, NY + 2, CO, NZ), BF),
            pltpu.VMEM((CO * NX * NY, NZ), F32),
            pltpu.VMEM((CI * NX * NY, NZ), F32),
        ],
        8, 1, 4 * 10**9,
    )(sy, *neighbours(dfirst, dlast, edge), bwd, act)
    whole = lax.axis_size("plane") * lax.axis_size(GROUP) * NX * NY * NZ
    norm = (1.0 / jnp.sqrt(jnp.float32(whole))).reshape(1)
    w, b = call(finish, (o((27 * CI, CO), F32), o((1, CO), F32)), (), 2, 1, 10**8)(norm, summed)
    wgrad = jnp.transpose(w.reshape(3, 3, 3, CI, CO), (4, 3, 0, 1, 2))
    return out[None], grad[None], wgrad, b.reshape(CO)


def solution(mesh):
    cores = 2
    samp, sx, sy = mesh.devices.shape
    mesh = Mesh(mesh.devices.reshape(samp // cores, cores, sx, sy), ("plane", "core", "sx", "sy"))
    spec = P(SAMP, None, "sx", "sy", None)
    return jax.shard_map(
        per_device, mesh=mesh, in_specs=(spec, P(), P(), spec), out_specs=(spec, spec, P(), P()), check_vma=False
    )
```

time: 116 us -> 93 us (0.80)
  the two profiles are of different devices: /device:TPU:2 before, /device:TPU:8 now
where the time goes in v2:
time: 93 us; the launch traced here: 92.5 us
  starting transfers between devices  63.9 us (69%)
  waiting for transfers between devices  17.5 us (19%)
  Pallas kernels  6.28 us (7%)
  local copies, waits for them, and re-layouts  3.87 us (4%)
    all_to_all x3, starting transfers between devices, everywhere(): return lax.all_to_all(blocks, axis, 0, 0, tiled=True)  28.3 us
    ppermute x2, starting transfers between devices, neighbours(): lax.ppermute(jnp.concatenate([lo, row, hi], axis=0), 'sy', [(0, 1), (1, 0)])  24.5 us
    all_to_all x3, waiting for transfers between devices, everywhere(): return lax.all_to_all(blocks, axis, 0, 0, tiled=True)  13 us
    ppermute x2, starting transfers between devices, neighbours(): before = lax.ppermute(last, 'sx', up)  8.46 us
    pallas_call x6, Pallas kernels, run(): return inner(*args[:smem], *near)  6.28 us
    ppermute x2, waiting for transfers between devices, neighbours(): after = lax.ppermute(first, 'sx', down)  3.25 us
    ppermute x2, starting transfers between devices, neighbours(): after = lax.ppermute(first, 'sx', down)  2.58 us
    unnamed x8, local copies, waits for them, and re-layouts  2.52 us
  transfers between devices with their start and end apart: 9, of which 6 were waited for; matrix products, arithmetic and copies ran while one was open for 2% of the time, Pallas kernels for 4%

profile of v2, /device:TPU:8, one launch (start us, length us, event | category | flops | bytes accessed | tf_op | source)
XLA Modules:
  0.0 92.5 jit_solution(716235509889071773)
XLA Ops:
  0.6 0.0 copy-start
  0.6 0.0 copy-start.2
  0.7 0.9 %copy-done.2 = bf16[1,32,2,8,128]{4,3,2,1,0:T(8,128)(2,1)S(1)} copy-done((bf16[1,32,2,8,128]{4,3,2,1,0:T(8,128)(2,1)S(1)}, bf16[1,32,2,8,128]{4,3,2,1,0:T(8,128)(2,1)}, u32[]{:S(2)}) %copy-start.2) | copy-done | bytes 131096
  1.6 0.1 shard_map.75
  1.7 4.3 %collective-permute-start = (bf16[8,32,128]{2,1,0:T(8,128)(2,1)S(1)}, bf16[8,32,128]{2,1,0:T(8,128)(2,1)S(1)}, u32[]{:S(2)}, u32[]{:S(2)}) collective-permute-start(bf16[8,32,128]{2,1,0:T(8,128)(2,1)S(1)} %get-tuple-element.24.hi_ref), channel_id=1, source_target_pairs={{0,2},{2,4},{4,6},{6,8},{8,10},{1,3},{3,5},{5,7},{7,9},{9,11},{12,... | collective-permute-start | bytes 196616 | tf_op jit(solution)/shard_map/ppermute | solution.py:254
  6.0 1.3 %collective-permute-start.1 = (bf16[8,32,128]{2,1,0:T(8,128)(2,1)S(1)}, bf16[8,32,128]{2,1,0:T(8,128)(2,1)S(1)}, u32[]{:S(2)}, u32[]{:S(2)}) collective-permute-start(bf16[8,32,128]{2,1,0:T(8,128)(2,1)S(1)} %get-tuple-element.25.lo_ref), channel_id=1, source_target_pairs={{2,0},{4,2},{6,4},{8,6},{10,8},{3,1},{5,3},{7,5},{9,7},{11,9},{14,... | collective-permute-start | bytes 196616 | tf_op jit(solution)/shard_map/ppermute | solution.py:255
  7.3 0.0 copy-start.3
  7.3 0.0 copy-done
  7.3 0.6 copy-done.3
  7.9 0.0 copy-start.1
  8.0 0.9 %copy-done.1 = bf16[64,32,3,3,3]{0,1,4,3,2:T(8,128)(2,1)S(1)} copy-done((bf16[64,32,3,3,3]{0,1,4,3,2:T(8,128)(2,1)S(1)}, bf16[64,32,3,3,3]{0,1,4,3,2:T(8,128)(2,1)}, u32[]{:S(2)}) %copy-start.1) | copy-done | bytes 110616
  8.9 0.3 shard_map.76
  9.2 0.0 collective-permute-done.before_ref
  9.3 3.3 %collective-permute-done.1.after_ref = bf16[8,32,128]{2,1,0:T(8,128)(2,1)S(1)} collective-permute-done((bf16[8,32,128]{2,1,0:T(8,128)(2,1)S(1)}, bf16[8,32,128]{2,1,0:T(8,128)(2,1)S(1)}, u32[]{:S(2)}, u32[]{:S(2)}) %collective-permute-start.1) | collective-permute-done | bytes 65568 | tf_op jit(solution)/shard_map/ppermute | solution.py:255
  12.5 14.5 %collective-permute-start.2 = (bf16[4,32,128]{2,1,0:T(8,128)(2,1)S(1)}, bf16[4,32,128]{2,1,0:T(8,128)(2,1)S(1)}, u32[]{:S(2)}, u32[]{:S(2)}) collective-permute-start(bf16[4,32,128]{2,1,0:T(8,128)(2,1)S(1)} %pad_maximum_fusion.1), channel_id=1, source_target_pairs={{0,1},{1,0},{2,3},{3,2},{4,5},{5,4},{6,7},{7,6},{8,9},{9,8},{10,11... | collective-permute-start | bytes 98312 | tf_op jit(solution)/shard_map/ppermute | solution.py:259
  27.0 1.8 %shard_map.77 = (bf16[16,64,128]{2,1,0:T(8,128)(2,1)S(1)}, bf16[8,64,128]{2,1,0:T(8,128)(2,1)S(1)}, bf16[8,64,128]{2,1,0:T(8,128)(2,1)S(1)}, f32[304,256]{1,0:T(8,128)S(1)}) custom-call(s32[1]{0:T(128)} %bitcast.sy_ref, bf16[8,32,128]{2,1,0:T(8,128)(2,1)S(1)} %collective-permute-done.before_ref, bf16[8,32,128]{2,1,0:T(8,128)(2,1)S(1)} %get-tuple-element.25.lo_ref, ...), custom_call_target="tpu_custom_call" | custom-call | flops 3000000000 | bytes 1048576 | tf_op jit(solution)/shard_map/pallas_call | solution.py:33
  28.8 0.1 collective-permute-done.2.row_ref
  28.9 1.5 %shard_map.78 = (bf16[16,64,128]{2,1,0:T(8,128)(2,1)S(1)}, bf16[8,64,128]{2,1,0:T(8,128)(2,1)S(1)}, bf16[8,64,128]{2,1,0:T(8,128)(2,1)S(1)}, bf16[2,64,128]{2,1,0:T(8,128)(2,1)S(1)}, bf16[512,128]{1,0:T(8,128)(2,1)}) custom-call(s32[1]{0:T(128)} %bitcast.sy_ref, bf16[8,32,128]{2,1,0:T(8,128)(2,1)S(1)} %collective-permute-done.before_ref, ...), custom_call_target="tpu_custom_call" | custom-call | flops 1000000000 | bytes 1048576 | tf_op jit(solution)/shard_map/pallas_call | solution.py:33
  30.4 10.2 %all-to-all-start = ((bf16[32,16,128]{2,1,0:T(8,128)(2,1)}), bf16[32,16,128]{2,1,0:T(8,128)(2,1)S(1)}, u32[]{:S(2)}, u32[]{:S(2)}) async-start(bf16[32,16,128]{2,1,0:T(8,128)(2,1)} %bitcast.8), calls=%async_computation | async-start | bytes 262144 | tf_op jit(solution)/shard_map/all_to_all | solution.py:229
  40.6 4.2 %collective-permute-start.3 = (bf16[8,64,128]{2,1,0:T(8,128)(2,1)S(1)}, bf16[8,64,128]{2,1,0:T(8,128)(2,1)S(1)}, u32[]{:S(2)}, u32[]{:S(2)}) collective-permute-start(bf16[8,64,128]{2,1,0:T(8,128)(2,1)S(1)} %get-tuple-element.34.hi_ref), channel_id=1, source_target_pairs={{0,2},{2,4},{4,6},{6,8},{8,10},{1,3},{3,5},{5,7},{7,9},{9,11},{12,... | collective-permute-start | bytes 393224 | tf_op jit(solution)/shard_map/ppermute | solution.py:254
  44.8 1.3 %collective-permute-start.4 = (bf16[8,64,128]{2,1,0:T(8,128)(2,1)S(1)}, bf16[8,64,128]{2,1,0:T(8,128)(2,1)S(1)}, u32[]{:S(2)}, u32[]{:S(2)}) collective-permute-start(bf16[8,64,128]{2,1,0:T(8,128)(2,1)S(1)} %get-tuple-element.35.lo_ref), channel_id=1, source_target_pairs={{2,0},{4,2},{6,4},{8,6},{10,8},{3,1},{5,3},{7,5},{9,7},{11,9},{14,... | collective-permute-start | bytes 393224 | tf_op jit(solution)/shard_map/ppermute | solution.py:255
  46.1 1.2 %collective-permute-done.3.before_ref = bf16[8,64,128]{2,1,0:T(8,128)(2,1)S(1)} collective-permute-done((bf16[8,64,128]{2,1,0:T(8,128)(2,1)S(1)}, bf16[8,64,128]{2,1,0:T(8,128)(2,1)S(1)}, u32[]{:S(2)}, u32[]{:S(2)}) %collective-permute-start.3) | collective-permute-done | bytes 131104 | tf_op jit(solution)/shard_map/ppermute | solution.py:254
  47.3 2.9 %all-to-all-done = bf16[32,16,128]{2,1,0:T(8,128)(2,1)S(1)} async-done(((bf16[32,16,128]{2,1,0:T(8,128)(2,1)}), bf16[32,16,128]{2,1,0:T(8,128)(2,1)S(1)}, u32[]{:S(2)}, u32[]{:S(2)}) %all-to-all-start) | async-done | bytes 131104 | tf_op jit(solution)/shard_map/all_to_all | solution.py:229
  50.2 0.7 broadcast_in_dim.20
  50.8 11.1 %all-to-all-start.1 = ((bf16[24,16,128]{2,1,0:T(8,128)(2,1)}), bf16[24,16,128]{2,1,0:T(8,128)(2,1)S(1)}, u32[]{:S(2)}, u32[]{:S(2)}) async-start(bf16[24,16,128]{2,1,0:T(8,128)(2,1)} %broadcast_in_dim.20), calls=%async_computation.1 | async-start | bytes 196608 | tf_op jit(solution)/shard_map/all_to_all | solution.py:229
  61.9 0.0 collective-permute-done.4.after_ref
  62.0 10.1 %collective-permute-start.5 = (bf16[4,64,128]{2,1,0:T(8,128)(2,1)S(1)}, bf16[4,64,128]{2,1,0:T(8,128)(2,1)S(1)}, u32[]{:S(2)}, u32[]{:S(2)}) collective-permute-start(bf16[4,64,128]{2,1,0:T(8,128)(2,1)S(1)} %pad_maximum_fusion), channel_id=1, source_target_pairs={{0,1},{1,0},{2,3},{3,2},{4,5},{5,4},{6,7},{7,6},{8,9},{9,8},{10,11... | collective-permute-start | bytes 196616 | tf_op jit(solution)/shard_map/ppermute | solution.py:259
  72.0 2.2 %all-to-all-done.1 = bf16[24,16,128]{2,1,0:T(8,128)(2,1)S(1)} async-done(((bf16[24,16,128]{2,1,0:T(8,128)(2,1)}), bf16[24,16,128]{2,1,0:T(8,128)(2,1)S(1)}, u32[]{:S(2)}, u32[]{:S(2)}) %all-to-all-start.1) | async-done | bytes 98336 | tf_op jit(solution)/shard_map/all_to_all | solution.py:229
  74.3 0.7 broadcast_in_dim.21
  74.9 7.1 %all-to-all-start.2 = ((bf16[32,16,128]{2,1,0:T(8,128)(2,1)}), bf16[32,16,128]{2,1,0:T(8,128)(2,1)S(1)}, u32[]{:S(2)}, u32[]{:S(2)}) async-start(bf16[32,16,128]{2,1,0:T(8,128)(2,1)} %broadcast_in_dim.21), calls=%async_computation.2 | async-start | bytes 262144 | tf_op jit(solution)/shard_map/all_to_all | solution.py:229
  82.0 0.0 collective-permute-done.5.row_ref
  82.0 1.6 %shard_map.79 = (bf16[64,2,8,128]{3,2,1,0:T(8,128)(2,1)}, bf16[32,2,8,128]{3,2,1,0:T(8,128)(2,1)}) custom-call(s32[1]{0:T(128)} %bitcast.sy_ref, bf16[8,64,128]{2,1,0:T(8,128)(2,1)S(1)} %collective-permute-done.3.before_ref, bf16[8,64,128]{2,1,0:T(8,128)(2,1)S(1)} %get-tuple-element.35.lo_ref, bf16[8,64,128]{2,1,0:T(8,128)(2,1)S(1)} %get-tuple-element.34.hi_ref, ...), custom_call_target="tpu_custom_call" | custom-call | flops 4000000000 | bytes 1048576 | tf_op jit(solution)/shard_map/pallas_call | solution.py:33
  83.7 7.9 %all-to-all-done.2 = bf16[32,16,128]{2,1,0:T(8,128)(2,1)S(1)} async-done(((bf16[32,16,128]{2,1,0:T(8,128)(2,1)}), bf16[32,16,128]{2,1,0:T(8,128)(2,1)S(1)}, u32[]{:S(2)}, u32[]{:S(2)}) %all-to-all-start.2) | async-done | bytes 131104 | tf_op jit(solution)/shard_map/all_to_all | solution.py:229
  91.6 0.9 shard_map.80
  (8 shorter events, 0.1 us)
Async XLA Ops:
  0.6 6.7 %copy-start = (bf16[1,64,2,8,128]{4,3,2,1,0:T(8,128)(2,1)S(1)}, bf16[1,64,2,8,128]{4,3,2,1,0:T(8,128)(2,1)}, u32[]{:S(2)}) copy-start(bf16[1,64,2,8,128]{4,3,2,1,0:T(8,128)(2,1)} %param.7) | copy-start | bytes 786436
  0.6 0.9 %copy-start.2 = (bf16[1,32,2,8,128]{4,3,2,1,0:T(8,128)(2,1)S(1)}, bf16[1,32,2,8,128]{4,3,2,1,0:T(8,128)(2,1)}, u32[]{:S(2)}) copy-start(bf16[1,32,2,8,128]{4,3,2,1,0:T(8,128)(2,1)} %param.4) | copy-start | bytes 393220
  1.7 7.5 %collective-permute-start = (bf16[8,32,128]{2,1,0:T(8,128)(2,1)S(1)}, bf16[8,32,128]{2,1,0:T(8,128)(2,1)S(1)}, u32[]{:S(2)}, u32[]{:S(2)}) collective-permute-start(bf16[8,32,128]{2,1,0:T(8,128)(2,1)S(1)} %get-tuple-element.24.hi_ref), channel_id=1, source_target_pairs={{0,2},{2,4},{4,6},{6,8},{8,10},{1,3},{3,5},{5,7},{7,9},{9,11},{12,... | collective-permute-start | bytes 196616 | tf_op jit(solution)/shard_map/ppermute | solution.py:254
  6.0 6.5 %collective-permute-start.1 = (bf16[8,32,128]{2,1,0:T(8,128)(2,1)S(1)}, bf16[8,32,128]{2,1,0:T(8,128)(2,1)S(1)}, u32[]{:S(2)}, u32[]{:S(2)}) collective-permute-start(bf16[8,32,128]{2,1,0:T(8,128)(2,1)S(1)} %get-tuple-element.25.lo_ref), channel_id=1, source_target_pairs={{2,0},{4,2},{6,4},{8,6},{10,8},{3,1},{5,3},{7,5},{9,7},{11,9},{14,... | collective-permute-start | bytes 196616 | tf_op jit(solution)/shard_map/ppermute | solution.py:255
  7.3 0.7 copy-start.3
  7.9 0.9 %copy-start.1 = (bf16[64,32,3,3,3]{0,1,4,3,2:T(8,128)(2,1)S(1)}, bf16[64,32,3,3,3]{0,1,4,3,2:T(8,128)(2,1)}, u32[]{:S(2)}) copy-start(bf16[64,32,3,3,3]{0,1,4,3,2:T(8,128)(2,1)} %param.5) | copy-start | bytes 331780
  12.5 16.4 %collective-permute-start.2 = (bf16[4,32,128]{2,1,0:T(8,128)(2,1)S(1)}, bf16[4,32,128]{2,1,0:T(8,128)(2,1)S(1)}, u32[]{:S(2)}, u32[]{:S(2)}) collective-permute-start(bf16[4,32,128]{2,1,0:T(8,128)(2,1)S(1)} %pad_maximum_fusion.1), channel_id=1, source_target_pairs={{0,1},{1,0},{2,3},{3,2},{4,5},{5,4},{6,7},{7,6},{8,9},{9,8},{10,11... | collective-permute-start | bytes 98312 | tf_op jit(solution)/shard_map/ppermute | solution.py:259
  30.4 19.7 %all-to-all-start = ((bf16[32,16,128]{2,1,0:T(8,128)(2,1)}), bf16[32,16,128]{2,1,0:T(8,128)(2,1)S(1)}, u32[]{:S(2)}, u32[]{:S(2)}) async-start(bf16[32,16,128]{2,1,0:T(8,128)(2,1)} %bitcast.8), calls=%async_computation | async-start | bytes 262144 | tf_op jit(solution)/shard_map/all_to_all | solution.py:229
  40.6 6.7 %collective-permute-start.3 = (bf16[8,64,128]{2,1,0:T(8,128)(2,1)S(1)}, bf16[8,64,128]{2,1,0:T(8,128)(2,1)S(1)}, u32[]{:S(2)}, u32[]{:S(2)}) collective-permute-start(bf16[8,64,128]{2,1,0:T(8,128)(2,1)S(1)} %get-tuple-element.34.hi_ref), channel_id=1, source_target_pairs={{0,2},{2,4},{4,6},{6,8},{8,10},{1,3},{3,5},{5,7},{7,9},{9,11},{12,... | collective-permute-start | bytes 393224 | tf_op jit(solution)/shard_map/ppermute | solution.py:254
  44.8 17.1 %collective-permute-start.4 = (bf16[8,64,128]{2,1,0:T(8,128)(2,1)S(1)}, bf16[8,64,128]{2,1,0:T(8,128)(2,1)S(1)}, u32[]{:S(2)}, u32[]{:S(2)}) collective-permute-start(bf16[8,64,128]{2,1,0:T(8,128)(2,1)S(1)} %get-tuple-element.35.lo_ref), channel_id=1, source_target_pairs={{2,0},{4,2},{6,4},{8,6},{10,8},{3,1},{5,3},{7,5},{9,7},{11,9},{14,... | collective-permute-start | bytes 393224 | tf_op jit(solution)/shard_map/ppermute | solution.py:255
  50.8 23.4 %all-to-all-start.1 = ((bf16[24,16,128]{2,1,0:T(8,128)(2,1)}), bf16[24,16,128]{2,1,0:T(8,128)(2,1)S(1)}, u32[]{:S(2)}, u32[]{:S(2)}) async-start(bf16[24,16,128]{2,1,0:T(8,128)(2,1)} %broadcast_in_dim.20), calls=%async_computation.1 | async-start | bytes 196608 | tf_op jit(solution)/shard_map/all_to_all | solution.py:229
  62.0 20.1 %collective-permute-start.5 = (bf16[4,64,128]{2,1,0:T(8,128)(2,1)S(1)}, bf16[4,64,128]{2,1,0:T(8,128)(2,1)S(1)}, u32[]{:S(2)}, u32[]{:S(2)}) collective-permute-start(bf16[4,64,128]{2,1,0:T(8,128)(2,1)S(1)} %pad_maximum_fusion), channel_id=1, source_target_pairs={{0,1},{1,0},{2,3},{3,2},{4,5},{5,4},{6,7},{7,6},{8,9},{9,8},{10,11... | collective-permute-start | bytes 196616 | tf_op jit(solution)/shard_map/ppermute | solution.py:259
  74.9 16.6 %all-to-all-start.2 = ((bf16[32,16,128]{2,1,0:T(8,128)(2,1)}), bf16[32,16,128]{2,1,0:T(8,128)(2,1)S(1)}, u32[]{:S(2)}, u32[]{:S(2)}) async-start(bf16[32,16,128]{2,1,0:T(8,128)(2,1)} %broadcast_in_dim.21), calls=%async_computation.2 | async-start | bytes 262144 | tf_op jit(solution)/shard_map/all_to_all | solution.py:229

commit v3 on v2

--- a/solution.py
+++ b/solution.py
@@ -35,17 +35,17 @@
     return run
 
 
-def turn_volume(sy_ref, v_ref, lo_ref, hi_ref, edge_ref, buf):
+def turn_volume(sy_ref, v_ref, own_ref, edge_ref, buf):
     buf[...] = v_ref[...].astype(F32).reshape(CI * NX * NY, NZ)
-    for x, t_ref in enumerate((lo_ref, hi_ref)):
+    for x in range(NX):
         for y in range(NY):
-            t_ref[y] = buf[pl.ds(x * NY + y, CI, stride=NX * NY), :].astype(BF)
+            own_ref[x, y] = buf[pl.ds(x * NY + y, CI, stride=NX * NY), :].astype(BF)
     edge = (1 - sy_ref[0]) * (NY - 1)
     for x in range(NX):
-        edge_ref[x] = buf[pl.ds(x * NY + edge, CI, stride=NX * NY), :].astype(BF)
-
-
-def prepare(w_ref, b_ref, u_ref, fwd_ref, bwd_ref, t_ref, wide_ref, buf):
+        edge_ref[x] = own_ref[x, edge]
+
+
+def prepare(w_ref, b_ref, u_ref, fwd_ref, bwd_ref, lo_ref, hi_ref, wide_ref, buf):
     eye = lax.broadcasted_iota(jnp.int32, (CO, CO), 0) == lax.broadcasted_iota(jnp.int32, (CO, CO), 1)
     column = jnp.sum(jnp.where(eye, b_ref[...], 0.0), axis=1, keepdims=True)
     wide_ref[...] = jnp.broadcast_to(column, (CO, NZ))
@@ -63,20 +63,9 @@
                 (ab * 3 + c) * CI : (ab * 3 + c + 1) * CI, :
             ]
     buf[...] = u_ref[...].astype(F32).reshape(CO * NX * NY, NZ)
-    for p in range(NX * NY):
-        t_ref[p] = buf[pl.ds(p, CO, stride=NX * NY), :].astype(BF)
-
-
-def fill(ext, sy, planes, rows):
-    for x, plane in enumerate(planes):
-        for y in range(NY):
-            ext[x, y + 1] = plane[y]
-    far = (1 - sy) * (NY + 1)
-    near = sy * (NY + 1)
-    nothing = jnp.zeros(ext.shape[2:], BF)
-    for x in range(4):
-        ext[x, near] = nothing
-        ext[x, far] = rows[x]
+    for y in range(NY):
+        lo_ref[y] = buf[pl.ds(y, CO, stride=NX * NY), :].astype(BF)
+        hi_ref[y] = buf[pl.ds(NY + y, CO, stride=NX * NY), :].astype(BF)
 
 
 def window(ext, x, y, channels):
@@ -97,7 +86,7 @@
     return jnp.where(lane == NZ - 1, 0.0, pltpu.roll(v, NZ - 1, 1))
 
 
-def two_rows(ext, x, y, at_y, fwd_ref, up_ref, bias_ref, act_ref, delta_refs):
+def two_rows(ext, x, y, at_y, first_x, fwd_ref, ups, bias_ref, acts, deltas):
     ones = jnp.ones((16, 2 * NZ), BF)
     none = jnp.zeros((CO, 2 * NZ), BF)
     first, second = window(ext, x, y, CI)
@@ -116,10 +105,14 @@
         r = 1.0 / (1.0 + e)
         sig = jnp.where(pre >= 0, r, e * r)
         soft = jnp.maximum(pre, 0.0) + jnp.log1p(e)
-        p = x * NY + at_y + k
-        act_ref[p] = (0.3 * pre + 0.7 * soft).astype(BF)
-        d = (up_ref[p].astype(F32) * (0.3 + 0.7 * sig)).astype(BF)
-        delta_refs[x][at_y + k] = d
+        act = 0.3 * pre + 0.7 * soft
+        grad = ups[x][at_y + k].astype(F32) * (0.3 + 0.7 * sig)
+        if x == 0:
+            act = jnp.where(first_x, act, 0.0)
+            grad = jnp.where(first_x, grad, 0.0)
+        acts[x][at_y + k] = act.astype(BF)
+        d = grad.astype(BF)
+        deltas[x][at_y + k] = d
         wide = d.astype(F32)
         shifted[0].append(moved(wide, -1).astype(BF))
         shifted[1].append(d)
@@ -129,50 +122,60 @@
     return lax.dot_general(left, right, NT_DIMS, preferred_element_type=F32)
 
 
+def places(send_ref, keep_ref):
+    acts = (keep_ref.at[1], keep_ref.at[2], send_ref.at[2])
+    return acts, (keep_ref.at[0], send_ref.at[0], send_ref.at[1])
+
+
 def forward_near(
-    sy_ref, before_ref, lo_ref, hi_ref, after_ref, fwd_ref, up_ref, bias_ref,
-    act_ref, dlo_ref, dhi_ref, acc, ext,
+    sy_ref, sx_ref, own_ref, next_ref, fwd_ref, lo_ref, hi_ref, up_ref, bias_ref,
+    send_ref, keep_ref, acc, ext,
 ):
     sy = sy_ref[0]
-    for x, plane in enumerate((before_ref, lo_ref, hi_ref, after_ref)):
+    ext[0] = jnp.zeros(ext.shape[1:], BF)
+    for x, plane in enumerate((own_ref.at[0], own_ref.at[1], next_ref.at[0], next_ref.at[1])):
         for y in range(NY):
-            ext[x, y + 1] = plane[y]
-        ext[x, sy * (NY + 1)] = jnp.zeros(ext.shape[2:], BF)
-        ext[x, (1 - sy) * (NY + 1)] = jnp.zeros(ext.shape[2:], BF)
-    for x in range(NX):
+            ext[x + 1, y + 1] = plane[y]
+        ext[x + 1, sy * (NY + 1)] = jnp.zeros(ext.shape[2:], BF)
+        ext[x + 1, (1 - sy) * (NY + 1)] = jnp.zeros(ext.shape[2:], BF)
+    acts, deltas = places(send_ref, keep_ref)
+    ups = (lo_ref, hi_ref, up_ref)
+    far = (1 - sy) * (NY - 2)
+    for x in range(NX + 1):
         for j in range(NY // 2 - 1):
             y = 2 * j + 2 * sy
-            part = two_rows(ext, x, y, y, fwd_ref, up_ref, bias_ref, act_ref, (dlo_ref, dhi_ref))
+            part = two_rows(ext, x, y, y, sx_ref[0] == 0, fwd_ref, ups, bias_ref, acts, deltas)
             if x + j:
                 acc[...] += part
             else:
                 acc[...] = part
-        far = (1 - sy) * (NY - 2)
         for k in range(2):
-            act_ref[x * NY + far + k] = jnp.zeros((CO, NZ), BF)
-            (dlo_ref, dhi_ref)[x][far + k] = jnp.zeros((CO, NZ), BF)
+            acts[x][far + k] = jnp.zeros((CO, NZ), BF)
+            deltas[x][far + k] = jnp.zeros((CO, NZ), BF)
 
 
 def forward_far(
-    sy_ref, before_ref, lo_ref, hi_ref, after_ref, row_ref, fwd_ref, up_ref, bias_ref,
-    act_in, dlo_in, dhi_in, acc_in, act_ref, dlo_ref, dhi_ref, edge_ref, sum_ref, ext, acc,
+    sy_ref, sx_ref, own_ref, next_ref, row_ref, fwd_ref, lo_ref, hi_ref, up_ref, bias_ref, send_in, keep_in, acc_in,
+    send_ref, keep_ref, edge_ref, sum_ref, ext, acc,
 ):
     sy = sy_ref[0]
-    act_ref[...] = act_in[...]
-    dlo_ref[...] = dlo_in[...]
-    dhi_ref[...] = dhi_in[...]
-    rows = row_ref
-    for x, plane in enumerate((before_ref, lo_ref, hi_ref, after_ref)):
+    send_ref[...] = send_in[...]
+    keep_ref[...] = keep_in[...]
+    ext[0] = jnp.zeros(ext.shape[1:], BF)
+    for x, plane in enumerate((own_ref.at[0], own_ref.at[1], next_ref.at[0], next_ref.at[1])):
         for y in range(3):
-            ext[x, sy + y] = plane[(1 - sy) * (NY - 3) + y]
-        ext[x, 3 * (1 - sy)] = rows[x]
+            ext[x + 1, sy + y] = plane[(1 - sy) * (NY - 3) + y]
+        ext[x + 1, 3 * (1 - sy)] = row_ref[x]
+    acts, deltas = places(send_ref, keep_ref)
+    ups = (lo_ref, hi_ref, up_ref)
     far = (1 - sy) * (NY - 2)
     acc[...] = acc_in[...]
-    for x in range(NX):
-        acc[...] += two_rows(ext, x, 0, far, fwd_ref, up_ref, bias_ref, act_ref, (dlo_ref, dhi_ref))
+    for x in range(NX + 1):
+        acc[...] += two_rows(ext, x, 0, far, sx_ref[0] == 0, fwd_ref, ups, bias_ref, acts, deltas)
     edge = (1 - sy) * (NY - 1)
-    edge_ref[0] = dlo_ref[edge]
-    edge_ref[1] = dhi_ref[edge]
+    edge_ref[0] = jnp.zeros((CO, NZ), BF)
+    for x in range(NX + 1):
+        edge_ref[x + 1] = deltas[x][edge]
     n = 9 * CI
     sum_ref[0:n, :] = acc[0:n, 0:NZ].astype(sum_ref.dtype)
     half = n // 2
@@ -183,14 +186,25 @@
     sum_ref[n + half + 8 :, :] = jnp.zeros((ROWS - n - half - 8, NZ), sum_ref.dtype)
 
 
+def plus(a, b):
+    return (a.astype(F32) + b.astype(F32)).astype(BF)
+
+
 def backward(
-    sy_ref, before_ref, lo_ref, hi_ref, after_ref, row_ref, bwd_ref, act_ref,
-    out_ref, grad_ref, ext, wide, narrow,
+    sy_ref, got_ref, send_ref, keep_ref, row_ref, bwd_ref, out_ref, grad_ref, ext, wide, narrow,
 ):
-    for p in range(NX * NY):
-        wide[pl.ds(p, CO, stride=NX * NY), :] = act_ref[p].astype(F32)
+    sy = sy_ref[0]
+    for y in range(NY):
+        wide[pl.ds(y, CO, stride=NX * NY), :] = got_ref[2, y].astype(F32) + keep_ref[1, y].astype(F32)
+        wide[pl.ds(NY + y, CO, stride=NX * NY), :] = keep_ref[2, y].astype(F32)
+        ext[0, y + 1] = got_ref[0, y]
+        ext[1, y + 1] = plus(got_ref[1, y], keep_ref[0, y])
+        ext[2, y + 1] = send_ref[0, y]
+        ext[3, y + 1] = send_ref[1, y]
     out_ref[...] = wide[...].reshape(CO, NX, NY, NZ).astype(BF)
-    fill(ext, sy_ref[0], (before_ref, lo_ref, hi_ref, after_ref), row_ref)
+    for x in range(4):
+        ext[x, sy * (NY + 1)] = jnp.zeros(ext.shape[2:], BF)
+        ext[x, (1 - sy) * (NY + 1)] = row_ref[x]
     for x in range(NX):
         for y in range(0, NY, 2):
             first, second = window(ext, x, y, CO)
@@ -247,45 +261,46 @@
     return share.reshape(ROWS, NZ)
 
 
-def neighbours(first, last, row):
+def per_device(volume, kernel, bias, upstream):
+    s = pltpu.VMEM
     n = lax.axis_size("sx")
-    up = [(i, i + 1) for i in range(n - 1)]
-    down = [(j, i) for i, j in up]
-    before = lax.ppermute(last, "sx", up)
-    after = lax.ppermute(first, "sx", down)
+    up_line = [(i, i + 1) for i in range(n - 1)]
+    down_line = [(j, i) for i, j in up_line]
+    swap = [(0, 1), (1, 0)]
+    sy = lax.axis_index("sy").astype(jnp.int32).reshape(1)
+    sx = lax.axis_index("sx").astype(jnp.int32).reshape(1)
     here = (1 - lax.axis_index("sy")) * (NY - 1)
-    lo = lax.dynamic_index_in_dim(before, here, 0, keepdims=True)
-    hi = lax.dynamic_index_in_dim(after, here, 0, keepdims=True)
-    swapped = lax.ppermute(jnp.concatenate([lo, row, hi], axis=0), "sy", [(0, 1), (1, 0)])
-    return before, first, last, after, swapped
-
-
-def per_device(volume, kernel, bias, upstream, dt=BF):
-    s = pltpu.VMEM
-    sy = lax.axis_index("sy").astype(jnp.int32).reshape(1)
     taps = jnp.transpose(kernel, (2, 3, 4, 1, 0)).reshape(27 * CI, CO)
-    first, last, row = call(
-        turn_volume,
-        (s((NY, CI, NZ), BF), s((NY, CI, NZ), BF), s((NX, CI, NZ), BF)),
+    own, row = call(
+        turn_volume, (s((NX, NY, CI, NZ), BF), s((NX, CI, NZ), BF)),
         [pltpu.VMEM((CI * NX * NY, NZ), F32)], 2, 1, 10**8,
     )(sy, volume[0])
-    fwd, bwd, up, bias_wide = call(
+    after = lax.ppermute(own, "sx", down_line)
+    fwd, bwd, lo, hi, bias_wide = call(
         prepare,
-        (s((3 * CO, 9 * CI), BF), s((3 * CI, 9 * CO), BF), s((NX * NY, CO, NZ), BF), s((CO, NZ), F32)),
+        (
+            s((3 * CO, 9 * CI), BF), s((3 * CI, 9 * CO), BF), s((NY, CO, NZ), BF), s((NY, CO, NZ), BF),
+            s((CO, NZ), F32),
+        ),
         [pltpu.VMEM((CO * NX * NY, NZ), F32)], 3, 0, 10**9,
     )(taps, bias.reshape(1, CO), upstream[0])
-    around = list(neighbours(first, last, row))
-    shapes = (s((NX * NY, CO, NZ), BF), s((NY, CO, NZ), BF), s((NY, CO, NZ), BF))
+    up = lax.ppermute(lo, "sx", down_line)
+    edges = lax.dynamic_index_in_dim(after, here, 1, keepdims=False)
+    swapped = lax.ppermute(jnp.concatenate([row, edges], axis=0), "sy", swap)
+    parts = (s((3, NY, CO, NZ), BF), s((3, NY, CO, NZ), BF))
     sums = (9 * CI + 16, 2 * NZ)
     early = call(
-        forward_near, (*shapes, s(sums, F32)),
-        [pltpu.VMEM((4, NY + 2, CI, NZ), BF)], 8, 1, 3 * 10**9,
-    )(sy, *around[:4], fwd, up, bias_wide)
-    act, dfirst, dlast, edge, part = call(
-        forward_far, (*shapes, s((NX, CO, NZ), BF), s((ROWS, NZ), dt)),
-        [pltpu.VMEM((4, 4, CI, NZ), BF), pltpu.VMEM(sums, F32)], 13, 1, 10**9,
-    )(sy, *around, fwd, up, bias_wide, *early)
+        forward_near, (*parts, s(sums, F32)), [pltpu.VMEM((5, NY + 2, CI, NZ), BF)], 9, 2, 3 * 10**9,
+    )(sy, sx, own, after, fwd, lo, hi, up, bias_wide)
+    send, keep, edge, part = call(
+        forward_far, (*parts, s((4, CO, NZ), BF), s((ROWS, NZ), BF)),
+        [pltpu.VMEM((5, 4, CI, NZ), BF), pltpu.VMEM(sums, F32)], 13, 2, 10**9,
+    )(sy, sx, own, after, swapped, fwd, lo, hi, up, bias_wide, *early)
+    got = lax.ppermute(send, "sx", up_line)
     summed = reduced(part)
+    edges = lax.dynamic_index_in_dim(got[:2], here, 1, keepdims=False)
+    edges = edge + jnp.concatenate([edges, jnp.zeros_like(edges)], axis=0)
+    swapped = lax.ppermute(edges, "sy", swap)
     o = jax.ShapeDtypeStruct
     out, grad = call(
         backward,
@@ -295,8 +310,8 @@
             pltpu.VMEM((CO * NX * NY, NZ), F32),
             pltpu.VMEM((CI * NX * NY, NZ), F32),
         ],
-        8, 1, 4 * 10**9,
-    )(sy, *neighbours(dfirst, dlast, edge), bwd, act)
+        6, 1, 4 * 10**9,
+    )(sy, got, send, keep, swapped, bwd)
     whole = lax.axis_size("plane") * lax.axis_size(GROUP) * NX * NY * NZ
     norm = (1.0 / jnp.sqrt(jnp.float32(whole))).reshape(1)
     w, b = call(finish, (o((27 * CI, CO), F32), o((1, CO), F32)), (), 2, 1, 10**8)(norm, summed)

time: 93 us -> 91.9 us (0.988)
  blocking collectives: 0 us -> 19.5 us
  starting transfers between devices: 63.9 us -> 47.1 us
  waiting for transfers between devices: 17.5 us -> 13.4 us
    all_to_all x0 -> x1, blocking collectives: none -> 19.5 us  [everywhere(): return lax.all_to_all(blocks, axis, 0, 0, tiled=True)]
    all_to_all x3 -> x2, starting transfers between devices: 28.3 us -> 15.3 us  [everywhere(): return lax.all_to_all(blocks, axis, 0, 0, tiled=True)]
    ppermute x6 -> x5, starting transfers between devices: 35.6 us -> 31.8 us  [the longest x1 14.8 us: per_device(): swapped = lax.ppermute(jnp.concatenate([row, edges], axis=0), 'sy', swap)]
    all_to_all x3 -> x2, waiting for transfers between devices: 13 us -> 10.1 us  [everywhere(): return lax.all_to_all(blocks, axis, 0, 0, tiled=True)]
    ppermute x6 -> x5, waiting for transfers between devices: 4.53 us -> 3.23 us  [the longest x1 3.22 us: per_device(): after = lax.ppermute(own, 'sx', down_line)]
  transfers between devices with their start and end apart: 9 -> 7, of which waited for: 6 -> 3; matrix products, arithmetic and copies ran while one was open for 2% -> 2% of each run, Pallas kernels for 4% -> 5%
where the time goes in v3:
time: 91.9 us; the launch traced here: 91.4 us
  starting transfers between devices  47.1 us (51%)
  blocking collectives  19.5 us (21%)
  waiting for transfers between devices  13.4 us (15%)
  Pallas kernels  6.67 us (7%)
  local copies, waits for them, and re-layouts  3.88 us (4%)
    all_to_all x1, blocking collectives, everywhere(): return lax.all_to_all(blocks, axis, 0, 0, tiled=True)  19.5 us
    all_to_all x2, starting transfers between devices, everywhere(): return lax.all_to_all(blocks, axis, 0, 0, tiled=True)  15.3 us
    ppermute x1, starting transfers between devices, per_device(): swapped = lax.ppermute(jnp.concatenate([row, edges], axis=0), 'sy', swap)  14.8 us
    all_to_all x2, waiting for transfers between devices, everywhere(): return lax.all_to_all(blocks, axis, 0, 0, tiled=True)  10.1 us
    ppermute x1, starting transfers between devices, per_device(): swapped = lax.ppermute(edges, 'sy', swap)  10.1 us
    pallas_call x6, Pallas kernels, run(): return inner(*args[:smem], *near)  6.67 us
    ppermute x1, starting transfers between devices, per_device(): got = lax.ppermute(send, 'sx', up_line)  4.27 us
    ppermute x1, waiting for transfers between devices, per_device(): after = lax.ppermute(own, 'sx', down_line)  3.22 us
  transfers between devices with their start and end apart: 7, of which 3 were waited for; matrix products, arithmetic and copies ran while one was open for 2% of the time, Pallas kernels for 5%

profile of v3, /device:TPU:8, one launch (start us, length us, event | category | flops | bytes accessed | tf_op | source)
XLA Modules:
  0.0 91.4 jit_solution(7833790908207971565)
XLA Ops:
  0.6 0.0 copy-start
  0.6 0.0 copy-start.2
  0.7 0.9 %copy-done.2 = bf16[1,32,2,8,128]{4,3,2,1,0:T(8,128)(2,1)S(1)} copy-done((bf16[1,32,2,8,128]{4,3,2,1,0:T(8,128)(2,1)S(1)}, bf16[1,32,2,8,128]{4,3,2,1,0:T(8,128)(2,1)}, u32[]{:S(2)}) %copy-start.2) | copy-done | bytes 131096
  1.6 0.1 shard_map.75
  1.7 1.3 %collective-permute-start = (bf16[2,8,32,128]{3,2,1,0:T(8,128)(2,1)S(1)}, bf16[2,8,32,128]{3,2,1,0:T(8,128)(2,1)S(1)}, u32[]{:S(2)}, u32[]{:S(2)}) collective-permute-start(bf16[2,8,32,128]{3,2,1,0:T(8,128)(2,1)S(1)} %get-tuple-element.22.own_ref), channel_id=1, source_target_pairs={{2,0},{4,2},{6,4},{8,6},{10,8},{3,1},{5,3},{7,5},{9,7},{11,9},{14,... | collective-permute-start | bytes 393224 | tf_op jit(solution)/shard_map/ppermute | solution.py:278
  3.0 0.0 copy-start.3
  3.0 0.0 copy-done
  3.0 0.6 copy-done.3
  3.6 0.0 copy-start.1
  3.7 0.9 %copy-done.1 = bf16[64,32,3,3,3]{0,1,4,3,2:T(8,128)(2,1)S(1)} copy-done((bf16[64,32,3,3,3]{0,1,4,3,2:T(8,128)(2,1)S(1)}, bf16[64,32,3,3,3]{0,1,4,3,2:T(8,128)(2,1)}, u32[]{:S(2)}) %copy-start.1) | copy-done | bytes 110616
  4.6 0.3 shard_map.76
  4.9 1.3 %collective-permute-start.2 = (bf16[8,64,128]{2,1,0:T(8,128)(2,1)S(1)}, bf16[8,64,128]{2,1,0:T(8,128)(2,1)S(1)}, u32[]{:S(2)}, u32[]{:S(2)}) collective-permute-start(bf16[8,64,128]{2,1,0:T(8,128)(2,1)S(1)} %get-tuple-element.25.lo_ref), channel_id=1, source_target_pairs={{2,0},{4,2},{6,4},{8,6},{10,8},{3,1},{5,3},{7,5},{9,7},{11,9},{14,... | collective-permute-start | bytes 393224 | tf_op jit(solution)/shard_map/ppermute | solution.py:287
  6.2 3.2 %collective-permute-done.next_ref = bf16[2,8,32,128]{3,2,1,0:T(8,128)(2,1)S(1)} collective-permute-done((bf16[2,8,32,128]{3,2,1,0:T(8,128)(2,1)S(1)}, bf16[2,8,32,128]{3,2,1,0:T(8,128)(2,1)S(1)}, u32[]{:S(2)}, u32[]{:S(2)}) %collective-permute-start) | collective-permute-done | bytes 131104 | tf_op jit(solution)/shard_map/ppermute | solution.py:278
  9.5 14.8 %collective-permute-start.1 = (bf16[4,32,128]{2,1,0:T(8,128)(2,1)S(1)}, bf16[4,32,128]{2,1,0:T(8,128)(2,1)S(1)}, u32[]{:S(2)}, u32[]{:S(2)}) collective-permute-start(bf16[4,32,128]{2,1,0:T(8,128)(2,1)S(1)} %pad_maximum_fusion), channel_id=1, source_target_pairs={{0,1},{1,0},{2,3},{3,2},{4,5},{5,4},{6,7},{7,6},{8,9},{9,8},{10,11... | collective-permute-start | bytes 98312 | tf_op jit(solution)/shard_map/ppermute | solution.py:289
  24.3 0.0 collective-permute-done.2.up_ref
  24.3 2.3 %shard_map.77 = (bf16[3,8,64,128]{3,2,1,0:T(8,128)(2,1)S(1)}, bf16[3,8,64,128]{3,2,1,0:T(8,128)(2,1)S(1)}, f32[304,256]{1,0:T(8,128)S(1)}) custom-call(s32[1]{0:T(128)} %bitcast.sy_ref, s32[1]{0:T(128)} %bitcast.1.sx_ref, bf16[2,8,32,128]{3,2,1,0:T(8,128)(2,1)S(1)} %get-tuple-element.22.own_ref, bf16[2,8,32,128]{3,2,1,0:T(8,128)(2,1)S(1)} %collective-permute-done.next_ref, ...), custom_call_target="tpu_custom_call" | custom-call | flops 3000000000 | bytes 1048576 | tf_op jit(solution)/shard_map/pallas_call | solution.py:33
  26.7 0.0 collective-permute-done.1.row_ref
  26.7 1.3 %shard_map.78 = (bf16[3,8,64,128]{3,2,1,0:T(8,128)(2,1)S(1)}, bf16[3,8,64,128]{3,2,1,0:T(8,128)(2,1)S(1)}, bf16[4,64,128]{2,1,0:T(8,128)(2,1)S(1)}, bf16[512,128]{1,0:T(8,128)(2,1)S(1)}) custom-call(s32[1]{0:T(128)} %bitcast.sy_ref, s32[1]{0:T(128)} %bitcast.1.sx_ref, bf16[2,8,32,128]{3,2,1,0:T(8,128)(2,1)S(1)} %get-tuple-element.22.own_ref, ...), custom_call_target="tpu_custom_call" | custom-call | flops 1000000000 | bytes 1048576 | tf_op jit(solution)/shard_map/pallas_call | solution.py:33
  28.0 4.3 %collective-permute-start.3 = (bf16[3,8,64,128]{3,2,1,0:T(8,128)(2,1)S(1)}, bf16[3,8,64,128]{3,2,1,0:T(8,128)(2,1)S(1)}, u32[]{:S(2)}, u32[]{:S(2)}) collective-permute-start(bf16[3,8,64,128]{3,2,1,0:T(8,128)(2,1)S(1)} %get-tuple-element.31.send_ref), channel_id=1, source_target_pairs={{0,2},{2,4},{4,6},{6,8},{8,10},{1,3},{3,5},{5,7},{7,9},{9,11},{12,... | collective-permute-start | bytes 1179656 | tf_op jit(solution)/shard_map/ppermute | solution.py:299
  32.3 19.5 %all_to_all.15 = bf16[32,16,128]{2,1,0:T(8,128)(2,1)S(1)} all-to-all(bf16[32,16,128]{2,1,0:T(8,128)(2,1)S(1)} %bitcast.21), channel_id=1, replica_groups=mesh['plane'=32,'core'=2,'sx'=6,'sy'=2] {'plane'}, dimensions={0} | all-to-all | bytes 262144 | tf_op jit(solution)/shard_map/all_to_all | solution.py:243
  51.9 0.7 broadcast_in_dim.10
  52.5 10.6 %all-to-all-start.1 = ((bf16[24,16,128]{2,1,0:T(8,128)(2,1)}), bf16[24,16,128]{2,1,0:T(8,128)(2,1)S(1)}, u32[]{:S(2)}, u32[]{:S(2)}) async-start(bf16[24,16,128]{2,1,0:T(8,128)(2,1)} %broadcast_in_dim.10), calls=%async_computation.1 | async-start | bytes 196608 | tf_op jit(solution)/shard_map/all_to_all | solution.py:243
  63.1 0.0 collective-permute-done.3.got_ref
  63.2 10.1 %collective-permute-start.4 = (bf16[4,64,128]{2,1,0:T(8,128)(2,1)S(1)}, bf16[4,64,128]{2,1,0:T(8,128)(2,1)S(1)}, u32[]{:S(2)}, u32[]{:S(2)}) collective-permute-start(bf16[4,64,128]{2,1,0:T(8,128)(2,1)S(1)} %pad_add_fusion), channel_id=1, source_target_pairs={{0,1},{1,0},{2,3},{3,2},{4,5},{5,4},{6,7},{7,6},{8,9},{9,8},{10,11... | collective-permute-start | bytes 196616 | tf_op jit(solution)/shard_map/ppermute | solution.py:303
  73.3 2.2 %all-to-all-done.1 = bf16[24,16,128]{2,1,0:T(8,128)(2,1)S(1)} async-done(((bf16[24,16,128]{2,1,0:T(8,128)(2,1)}), bf16[24,16,128]{2,1,0:T(8,128)(2,1)S(1)}, u32[]{:S(2)}, u32[]{:S(2)}) %all-to-all-start.1) | async-done | bytes 98336 | tf_op jit(solution)/shard_map/all_to_all | solution.py:243
  75.5 0.7 broadcast_in_dim.22
  76.2 4.7 %all-to-all-start.2 = ((bf16[32,16,128]{2,1,0:T(8,128)(2,1)}), bf16[32,16,128]{2,1,0:T(8,128)(2,1)S(1)}, u32[]{:S(2)}, u32[]{:S(2)}) async-start(bf16[32,16,128]{2,1,0:T(8,128)(2,1)} %broadcast_in_dim.22), calls=%async_computation.2 | async-start | bytes 262144 | tf_op jit(solution)/shard_map/all_to_all | solution.py:243
  80.9 0.0 collective-permute-done.4.row_ref
  80.9 1.7 %shard_map.79 = (bf16[64,2,8,128]{3,2,1,0:T(8,128)(2,1)}, bf16[32,2,8,128]{3,2,1,0:T(8,128)(2,1)}) custom-call(s32[1]{0:T(128)} %bitcast.sy_ref, bf16[3,8,64,128]{3,2,1,0:T(8,128)(2,1)S(1)} %collective-permute-done.3.got_ref, bf16[3,8,64,128]{3,2,1,0:T(8,128)(2,1)S(1)} %get-tuple-element.31.send_ref, bf16[3,8,64,128]{3,2,1,0:T(8,128)(2,1)S(1)} %get-tuple-element.32.keep_ref, ...), custom_call_target="tpu_custom_call" | custom-call | flops 4000000000 | bytes 1048576 | tf_op jit(solution)/shard_map/pallas_call | solution.py:33
  82.6 7.9 %all-to-all-done.2 = bf16[32,16,128]{2,1,0:T(8,128)(2,1)S(1)} async-done(((bf16[32,16,128]{2,1,0:T(8,128)(2,1)}), bf16[32,16,128]{2,1,0:T(8,128)(2,1)S(1)}, u32[]{:S(2)}, u32[]{:S(2)}) %all-to-all-start.2) | async-done | bytes 131104 | tf_op jit(solution)/shard_map/all_to_all | solution.py:243
  90.5 0.9 shard_map.80
  (7 shorter events, 0.1 us)
Async XLA Ops:
  0.6 2.4 %copy-start = (bf16[1,64,2,8,128]{4,3,2,1,0:T(8,128)(2,1)S(1)}, bf16[1,64,2,8,128]{4,3,2,1,0:T(8,128)(2,1)}, u32[]{:S(2)}) copy-start(bf16[1,64,2,8,128]{4,3,2,1,0:T(8,128)(2,1)} %param.7) | copy-start | bytes 786436
  0.6 0.9 %copy-start.2 = (bf16[1,32,2,8,128]{4,3,2,1,0:T(8,128)(2,1)S(1)}, bf16[1,32,2,8,128]{4,3,2,1,0:T(8,128)(2,1)}, u32[]{:S(2)}) copy-start(bf16[1,32,2,8,128]{4,3,2,1,0:T(8,128)(2,1)} %param.4) | copy-start | bytes 393220
  1.7 7.8 %collective-permute-start = (bf16[2,8,32,128]{3,2,1,0:T(8,128)(2,1)S(1)}, bf16[2,8,32,128]{3,2,1,0:T(8,128)(2,1)S(1)}, u32[]{:S(2)}, u32[]{:S(2)}) collective-permute-start(bf16[2,8,32,128]{3,2,1,0:T(8,128)(2,1)S(1)} %get-tuple-element.22.own_ref), channel_id=1, source_target_pairs={{2,0},{4,2},{6,4},{8,6},{10,8},{3,1},{5,3},{7,5},{9,7},{11,9},{14,... | collective-permute-start | bytes 393224 | tf_op jit(solution)/shard_map/ppermute | solution.py:278
  3.0 0.7 copy-start.3
  3.6 0.9 %copy-start.1 = (bf16[64,32,3,3,3]{0,1,4,3,2:T(8,128)(2,1)S(1)}, bf16[64,32,3,3,3]{0,1,4,3,2:T(8,128)(2,1)}, u32[]{:S(2)}) copy-start(bf16[64,32,3,3,3]{0,1,4,3,2:T(8,128)(2,1)} %param.5) | copy-start | bytes 331780
  4.9 19.4 %collective-permute-start.2 = (bf16[8,64,128]{2,1,0:T(8,128)(2,1)S(1)}, bf16[8,64,128]{2,1,0:T(8,128)(2,1)S(1)}, u32[]{:S(2)}, u32[]{:S(2)}) collective-permute-start(bf16[8,64,128]{2,1,0:T(8,128)(2,1)S(1)} %get-tuple-element.25.lo_ref), channel_id=1, source_target_pairs={{2,0},{4,2},{6,4},{8,6},{10,8},{3,1},{5,3},{7,5},{9,7},{11,9},{14,... | collective-permute-start | bytes 393224 | tf_op jit(solution)/shard_map/ppermute | solution.py:287
  9.5 17.2 %collective-permute-start.1 = (bf16[4,32,128]{2,1,0:T(8,128)(2,1)S(1)}, bf16[4,32,128]{2,1,0:T(8,128)(2,1)S(1)}, u32[]{:S(2)}, u32[]{:S(2)}) collective-permute-start(bf16[4,32,128]{2,1,0:T(8,128)(2,1)S(1)} %pad_maximum_fusion), channel_id=1, source_target_pairs={{0,1},{1,0},{2,3},{3,2},{4,5},{5,4},{6,7},{7,6},{8,9},{9,8},{10,11... | collective-permute-start | bytes 98312 | tf_op jit(solution)/shard_map/ppermute | solution.py:289
  28.0 35.1 %collective-permute-start.3 = (bf16[3,8,64,128]{3,2,1,0:T(8,128)(2,1)S(1)}, bf16[3,8,64,128]{3,2,1,0:T(8,128)(2,1)S(1)}, u32[]{:S(2)}, u32[]{:S(2)}) collective-permute-start(bf16[3,8,64,128]{3,2,1,0:T(8,128)(2,1)S(1)} %get-tuple-element.31.send_ref), channel_id=1, source_target_pairs={{0,2},{2,4},{4,6},{6,8},{8,10},{1,3},{3,5},{5,7},{7,9},{9,11},{12,... | collective-permute-start | bytes 1179656 | tf_op jit(solution)/shard_map/ppermute | solution.py:299
  52.5 22.9 %all-to-all-start.1 = ((bf16[24,16,128]{2,1,0:T(8,128)(2,1)}), bf16[24,16,128]{2,1,0:T(8,128)(2,1)S(1)}, u32[]{:S(2)}, u32[]{:S(2)}) async-start(bf16[24,16,128]{2,1,0:T(8,128)(2,1)} %broadcast_in_dim.10), calls=%async_computation.1 | async-start | bytes 196608 | tf_op jit(solution)/shard_map/all_to_all | solution.py:243
  63.2 17.7 %collective-permute-start.4 = (bf16[4,64,128]{2,1,0:T(8,128)(2,1)S(1)}, bf16[4,64,128]{2,1,0:T(8,128)(2,1)S(1)}, u32[]{:S(2)}, u32[]{:S(2)}) collective-permute-start(bf16[4,64,128]{2,1,0:T(8,128)(2,1)S(1)} %pad_add_fusion), channel_id=1, source_target_pairs={{0,1},{1,0},{2,3},{3,2},{4,5},{5,4},{6,7},{7,6},{8,9},{9,8},{10,11... | collective-permute-start | bytes 196616 | tf_op jit(solution)/shard_map/ppermute | solution.py:303
  76.2 14.3 %all-to-all-start.2 = ((bf16[32,16,128]{2,1,0:T(8,128)(2,1)}), bf16[32,16,128]{2,1,0:T(8,128)(2,1)S(1)}, u32[]{:S(2)}, u32[]{:S(2)}) async-start(bf16[32,16,128]{2,1,0:T(8,128)(2,1)} %broadcast_in_dim.22), calls=%async_computation.2 | async-start | bytes 262144 | tf_op jit(solution)/shard_map/all_to_all | solution.py:243

commit v4 on v3

--- a/solution.py
+++ b/solution.py
@@ -122,14 +122,14 @@
     return lax.dot_general(left, right, NT_DIMS, preferred_element_type=F32)
 
 
-def places(send_ref, keep_ref):
-    acts = (keep_ref.at[1], keep_ref.at[2], send_ref.at[2])
+def places(send_ref, keep_ref, last_ref):
+    acts = (keep_ref.at[1], keep_ref.at[2], last_ref)
     return acts, (keep_ref.at[0], send_ref.at[0], send_ref.at[1])
 
 
 def forward_near(
     sy_ref, sx_ref, own_ref, next_ref, fwd_ref, lo_ref, hi_ref, up_ref, bias_ref,
-    send_ref, keep_ref, acc, ext,
+    send_ref, keep_ref, last_ref, acc, ext,
 ):
     sy = sy_ref[0]
     ext[0] = jnp.zeros(ext.shape[1:], BF)
@@ -138,7 +138,7 @@
             ext[x + 1, y + 1] = plane[y]
         ext[x + 1, sy * (NY + 1)] = jnp.zeros(ext.shape[2:], BF)
         ext[x + 1, (1 - sy) * (NY + 1)] = jnp.zeros(ext.shape[2:], BF)
-    acts, deltas = places(send_ref, keep_ref)
+    acts, deltas = places(send_ref, keep_ref, last_ref)
     ups = (lo_ref, hi_ref, up_ref)
     far = (1 - sy) * (NY - 2)
     for x in range(NX + 1):
@@ -155,18 +155,19 @@
 
 
 def forward_far(
-    sy_ref, sx_ref, own_ref, next_ref, row_ref, fwd_ref, lo_ref, hi_ref, up_ref, bias_ref, send_in, keep_in, acc_in,
-    send_ref, keep_ref, edge_ref, sum_ref, ext, acc,
+    sy_ref, sx_ref, own_ref, next_ref, row_ref, fwd_ref, lo_ref, hi_ref, up_ref, bias_ref, send_in, keep_in,
+    last_in, acc_in, send_ref, keep_ref, last_ref, edge_ref, sum_ref, ext, acc,
 ):
     sy = sy_ref[0]
     send_ref[...] = send_in[...]
     keep_ref[...] = keep_in[...]
+    last_ref[...] = last_in[...]
     ext[0] = jnp.zeros(ext.shape[1:], BF)
     for x, plane in enumerate((own_ref.at[0], own_ref.at[1], next_ref.at[0], next_ref.at[1])):
         for y in range(3):
             ext[x + 1, sy + y] = plane[(1 - sy) * (NY - 3) + y]
         ext[x + 1, 3 * (1 - sy)] = row_ref[x]
-    acts, deltas = places(send_ref, keep_ref)
+    acts, deltas = places(send_ref, keep_ref, last_ref)
     ups = (lo_ref, hi_ref, up_ref)
     far = (1 - sy) * (NY - 2)
     acc[...] = acc_in[...]
@@ -191,11 +192,11 @@
 
 
 def backward(
-    sy_ref, got_ref, send_ref, keep_ref, row_ref, bwd_ref, out_ref, grad_ref, ext, wide, narrow,
+    sy_ref, got_ref, act_ref, send_ref, keep_ref, row_ref, bwd_ref, out_ref, grad_ref, ext, wide, narrow,
 ):
     sy = sy_ref[0]
     for y in range(NY):
-        wide[pl.ds(y, CO, stride=NX * NY), :] = got_ref[2, y].astype(F32) + keep_ref[1, y].astype(F32)
+        wide[pl.ds(y, CO, stride=NX * NY), :] = act_ref[y].astype(F32) + keep_ref[1, y].astype(F32)
         wide[pl.ds(NY + y, CO, stride=NX * NY), :] = keep_ref[2, y].astype(F32)
         ext[0, y + 1] = got_ref[0, y]
         ext[1, y + 1] = plus(got_ref[1, y], keep_ref[0, y])
@@ -287,20 +288,21 @@
     up = lax.ppermute(lo, "sx", down_line)
     edges = lax.dynamic_index_in_dim(after, here, 1, keepdims=False)
     swapped = lax.ppermute(jnp.concatenate([row, edges], axis=0), "sy", swap)
-    parts = (s((3, NY, CO, NZ), BF), s((3, NY, CO, NZ), BF))
+    parts = (s((2, NY, CO, NZ), BF), s((3, NY, CO, NZ), BF), s((NY, CO, NZ), BF))
     sums = (9 * CI + 16, 2 * NZ)
     early = call(
         forward_near, (*parts, s(sums, F32)), [pltpu.VMEM((5, NY + 2, CI, NZ), BF)], 9, 2, 3 * 10**9,
     )(sy, sx, own, after, fwd, lo, hi, up, bias_wide)
-    send, keep, edge, part = call(
+    send, keep, last, edge, part = call(
         forward_far, (*parts, s((4, CO, NZ), BF), s((ROWS, NZ), BF)),
-        [pltpu.VMEM((5, 4, CI, NZ), BF), pltpu.VMEM(sums, F32)], 13, 2, 10**9,
+        [pltpu.VMEM((5, 4, CI, NZ), BF), pltpu.VMEM(sums, F32)], 14, 2, 10**9,
     )(sy, sx, own, after, swapped, fwd, lo, hi, up, bias_wide, *early)
     got = lax.ppermute(send, "sx", up_line)
     summed = reduced(part)
-    edges = lax.dynamic_index_in_dim(got[:2], here, 1, keepdims=False)
+    edges = lax.dynamic_index_in_dim(got, here, 1, keepdims=False)
     edges = edge + jnp.concatenate([edges, jnp.zeros_like(edges)], axis=0)
     swapped = lax.ppermute(edges, "sy", swap)
+    act = lax.ppermute(last, "sx", up_line)
     o = jax.ShapeDtypeStruct
     out, grad = call(
         backward,
@@ -310,8 +312,8 @@
             pltpu.VMEM((CO * NX * NY, NZ), F32),
             pltpu.VMEM((CI * NX * NY, NZ), F32),
         ],
-        6, 1, 4 * 10**9,
-    )(sy, got, send, keep, swapped, bwd)
+        7, 1, 4 * 10**9,
+    )(sy, got, act, send, keep, swapped, bwd)
     whole = lax.axis_size("plane") * lax.axis_size(GROUP) * NX * NY * NZ
     norm = (1.0 / jnp.sqrt(jnp.float32(whole))).reshape(1)
     w, b = call(finish, (o((27 * CI, CO), F32), o((1, CO), F32)), (), 2, 1, 10**8)(norm, summed)

time: 91.9 us -> 92.7 us (level)
  blocking collectives: 19.5 us -> 0 us
  starting transfers between devices: 47.1 us -> 59.2 us
  waiting for transfers between devices: 13.4 us -> 20.9 us
    all_to_all x1 -> x0, blocking collectives: 19.5 us -> none  [everywhere(): return lax.all_to_all(blocks, axis, 0, 0, tiled=True)]
    all_to_all x2 -> x3, starting transfers between devices: 15.3 us -> 25.5 us  [everywhere(): return lax.all_to_all(blocks, axis, 0, 0, tiled=True)]
    all_to_all x2 -> x3, waiting for transfers between devices: 10.1 us -> 17.7 us  [everywhere(): return lax.all_to_all(blocks, axis, 0, 0, tiled=True)]
    ppermute x0 -> x1, starting transfers between devices: none -> 2.01 us  [per_device(): act = lax.ppermute(last, 'sx', up_line)]
  transfers between devices with their start and end apart: 7 -> 9, of which waited for: 3 -> 4; matrix products, arithmetic and copies ran while one was open for 2% -> 2% of each run, Pallas kernels for 5% -> 5%
where the time goes in v4:
time: 92.7 us; the launch traced here: 92.2 us
  starting transfers between devices  59.2 us (64%)
  waiting for transfers between devices  20.9 us (23%)
  Pallas kernels  7.32 us (8%)
  local copies, waits for them, and re-layouts  3.86 us (4%)
    all_to_all x3, starting transfers between devices, everywhere(): return lax.all_to_all(blocks, axis, 0, 0, tiled=True)  25.5 us
    all_to_all x3, waiting for transfers between devices, everywhere(): return lax.all_to_all(blocks, axis, 0, 0, tiled=True)  17.7 us
    ppermute x1, starting transfers between devices, per_device(): swapped = lax.ppermute(jnp.concatenate([row, edges], axis=0), 'sy', swap)  14.8 us
    ppermute x1, starting transfers between devices, per_device(): swapped = lax.ppermute(edges, 'sy', swap)  10.1 us
    pallas_call x6, Pallas kernels, run(): return inner(*args[:smem], *near)  7.32 us
    ppermute x1, starting transfers between devices, per_device(): got = lax.ppermute(send, 'sx', up_line)  4.25 us
    ppermute x1, waiting for transfers between devices, per_device(): after = lax.ppermute(own, 'sx', down_line)  3.22 us
    unnamed x8, local copies, waits for them, and re-layouts  2.52 us
  transfers between devices with their start and end apart: 9, of which 4 were waited for; matrix products, arithmetic and copies ran while one was open for 2% of the time, Pallas kernels for 5%

profile of v4, /device:TPU:8, one launch (start us, length us, event | category | flops | bytes accessed | tf_op | source)
XLA Modules:
  0.0 92.2 jit_solution(616051582844711981)
XLA Ops:
  0.6 0.0 copy-start
  0.6 0.0 copy-start.2
  0.7 0.9 %copy-done.2 = bf16[1,32,2,8,128]{4,3,2,1,0:T(8,128)(2,1)S(1)} copy-done((bf16[1,32,2,8,128]{4,3,2,1,0:T(8,128)(2,1)S(1)}, bf16[1,32,2,8,128]{4,3,2,1,0:T(8,128)(2,1)}, u32[]{:S(2)}) %copy-start.2) | copy-done | bytes 131096
  1.6 0.1 shard_map.75
  1.7 1.3 %collective-permute-start = (bf16[2,8,32,128]{3,2,1,0:T(8,128)(2,1)S(1)}, bf16[2,8,32,128]{3,2,1,0:T(8,128)(2,1)S(1)}, u32[]{:S(2)}, u32[]{:S(2)}) collective-permute-start(bf16[2,8,32,128]{3,2,1,0:T(8,128)(2,1)S(1)} %get-tuple-element.24.own_ref), channel_id=1, source_target_pairs={{2,0},{4,2},{6,4},{8,6},{10,8},{3,1},{5,3},{7,5},{9,7},{11,9},{14,... | collective-permute-start | bytes 393224 | tf_op jit(solution)/shard_map/ppermute | solution.py:279
  3.0 0.0 copy-start.3
  3.0 0.0 copy-done
  3.0 0.6 copy-done.3
  3.6 0.0 copy-start.1
  3.7 0.9 %copy-done.1 = bf16[64,32,3,3,3]{0,1,4,3,2:T(8,128)(2,1)S(1)} copy-done((bf16[64,32,3,3,3]{0,1,4,3,2:T(8,128)(2,1)S(1)}, bf16[64,32,3,3,3]{0,1,4,3,2:T(8,128)(2,1)}, u32[]{:S(2)}) %copy-start.1) | copy-done | bytes 110616
  4.6 0.3 shard_map.76
  4.9 1.3 %collective-permute-start.2 = (bf16[8,64,128]{2,1,0:T(8,128)(2,1)S(1)}, bf16[8,64,128]{2,1,0:T(8,128)(2,1)S(1)}, u32[]{:S(2)}, u32[]{:S(2)}) collective-permute-start(bf16[8,64,128]{2,1,0:T(8,128)(2,1)S(1)} %get-tuple-element.27.lo_ref), channel_id=1, source_target_pairs={{2,0},{4,2},{6,4},{8,6},{10,8},{3,1},{5,3},{7,5},{9,7},{11,9},{14,... | collective-permute-start | bytes 393224 | tf_op jit(solution)/shard_map/ppermute | solution.py:288
  6.2 3.2 %collective-permute-done.next_ref = bf16[2,8,32,128]{3,2,1,0:T(8,128)(2,1)S(1)} collective-permute-done((bf16[2,8,32,128]{3,2,1,0:T(8,128)(2,1)S(1)}, bf16[2,8,32,128]{3,2,1,0:T(8,128)(2,1)S(1)}, u32[]{:S(2)}, u32[]{:S(2)}) %collective-permute-start) | collective-permute-done | bytes 131104 | tf_op jit(solution)/shard_map/ppermute | solution.py:279
  9.5 14.8 %collective-permute-start.1 = (bf16[4,32,128]{2,1,0:T(8,128)(2,1)S(1)}, bf16[4,32,128]{2,1,0:T(8,128)(2,1)S(1)}, u32[]{:S(2)}, u32[]{:S(2)}) collective-permute-start(bf16[4,32,128]{2,1,0:T(8,128)(2,1)S(1)} %pad_maximum_fusion), channel_id=1, source_target_pairs={{0,1},{1,0},{2,3},{3,2},{4,5},{5,4},{6,7},{7,6},{8,9},{9,8},{10,11... | collective-permute-start | bytes 98312 | tf_op jit(solution)/shard_map/ppermute | solution.py:290
  24.3 0.0 collective-permute-done.2.up_ref
  24.3 2.3 %shard_map.77 = (bf16[2,8,64,128]{3,2,1,0:T(8,128)(2,1)S(1)}, bf16[3,8,64,128]{3,2,1,0:T(8,128)(2,1)S(1)}, bf16[8,64,128]{2,1,0:T(8,128)(2,1)S(1)}, f32[304,256]{1,0:T(8,128)S(1)}) custom-call(s32[1]{0:T(128)} %bitcast.sy_ref, s32[1]{0:T(128)} %bitcast.1.sx_ref, bf16[2,8,32,128]{3,2,1,0:T(8,128)(2,1)S(1)} %get-tuple-element.24.own_ref, ...), custom_call_target="tpu_custom_call" | custom-call | flops 3000000000 | bytes 1048576 | tf_op jit(solution)/shard_map/pallas_call | solution.py:33
  26.7 0.0 collective-permute-done.1.row_ref
  26.7 2.0 %shard_map.78 = (bf16[2,8,64,128]{3,2,1,0:T(8,128)(2,1)S(1)}, bf16[3,8,64,128]{3,2,1,0:T(8,128)(2,1)S(1)}, bf16[8,64,128]{2,1,0:T(8,128)(2,1)S(1)}, bf16[4,64,128]{2,1,0:T(8,128)(2,1)S(1)}, bf16[512,128]{1,0:T(8,128)(2,1)}) custom-call(s32[1]{0:T(128)} %bitcast.sy_ref, s32[1]{0:T(128)} %bitcast.1.sx_ref, ...), custom_call_target="tpu_custom_call" | custom-call | flops 1000000000 | bytes 1048576 | tf_op jit(solution)/shard_map/pallas_call | solution.py:33
  28.7 4.2 %collective-permute-start.3 = (bf16[2,8,64,128]{3,2,1,0:T(8,128)(2,1)S(1)}, bf16[2,8,64,128]{3,2,1,0:T(8,128)(2,1)S(1)}, u32[]{:S(2)}, u32[]{:S(2)}) collective-permute-start(bf16[2,8,64,128]{3,2,1,0:T(8,128)(2,1)S(1)} %get-tuple-element.34.send_ref), channel_id=1, source_target_pairs={{0,2},{2,4},{4,6},{6,8},{8,10},{1,3},{3,5},{5,7},{7,9},{9,11},{12,... | collective-permute-start | bytes 786440 | tf_op jit(solution)/shard_map/ppermute | solution.py:300
  32.9 10.2 %all-to-all-start = ((bf16[32,16,128]{2,1,0:T(8,128)(2,1)}), bf16[32,16,128]{2,1,0:T(8,128)(2,1)S(1)}, u32[]{:S(2)}, u32[]{:S(2)}) async-start(bf16[32,16,128]{2,1,0:T(8,128)(2,1)} %bitcast.11), calls=%async_computation | async-start | bytes 262144 | tf_op jit(solution)/shard_map/all_to_all | solution.py:244
  43.1 2.0 %collective-permute-start.4 = (bf16[8,64,128]{2,1,0:T(8,128)(2,1)S(1)}, bf16[8,64,128]{2,1,0:T(8,128)(2,1)S(1)}, u32[]{:S(2)}, u32[]{:S(2)}) collective-permute-start(bf16[8,64,128]{2,1,0:T(8,128)(2,1)S(1)} %get-tuple-element.35), channel_id=1, source_target_pairs={{0,2},{2,4},{4,6},{6,8},{8,10},{1,3},{3,5},{5,7},{7,9},{9,11},{12,... | collective-permute-start | bytes 393224 | tf_op jit(solution)/shard_map/ppermute | solution.py:305
  45.1 7.5 %all-to-all-done = bf16[32,16,128]{2,1,0:T(8,128)(2,1)S(1)} async-done(((bf16[32,16,128]{2,1,0:T(8,128)(2,1)}), bf16[32,16,128]{2,1,0:T(8,128)(2,1)S(1)}, u32[]{:S(2)}, u32[]{:S(2)}) %all-to-all-start) | async-done | bytes 131104 | tf_op jit(solution)/shard_map/all_to_all | solution.py:244
  52.7 0.7 broadcast_in_dim.10
  53.4 10.6 %all-to-all-start.1 = ((bf16[24,16,128]{2,1,0:T(8,128)(2,1)}), bf16[24,16,128]{2,1,0:T(8,128)(2,1)S(1)}, u32[]{:S(2)}, u32[]{:S(2)}) async-start(bf16[24,16,128]{2,1,0:T(8,128)(2,1)} %broadcast_in_dim.10), calls=%async_computation.1 | async-start | bytes 196608 | tf_op jit(solution)/shard_map/all_to_all | solution.py:244
  64.0 0.0 collective-permute-done.3.got_ref
  64.0 10.1 %collective-permute-start.5 = (bf16[4,64,128]{2,1,0:T(8,128)(2,1)S(1)}, bf16[4,64,128]{2,1,0:T(8,128)(2,1)S(1)}, u32[]{:S(2)}, u32[]{:S(2)}) collective-permute-start(bf16[4,64,128]{2,1,0:T(8,128)(2,1)S(1)} %pad_add_fusion), channel_id=1, source_target_pairs={{0,1},{1,0},{2,3},{3,2},{4,5},{5,4},{6,7},{7,6},{8,9},{9,8},{10,11... | collective-permute-start | bytes 196616 | tf_op jit(solution)/shard_map/ppermute | solution.py:304
  74.1 2.2 %all-to-all-done.1 = bf16[24,16,128]{2,1,0:T(8,128)(2,1)S(1)} async-done(((bf16[24,16,128]{2,1,0:T(8,128)(2,1)}), bf16[24,16,128]{2,1,0:T(8,128)(2,1)S(1)}, u32[]{:S(2)}, u32[]{:S(2)}) %all-to-all-start.1) | async-done | bytes 98336 | tf_op jit(solution)/shard_map/all_to_all | solution.py:244
  76.3 0.7 broadcast_in_dim.22
  77.0 4.7 %all-to-all-start.2 = ((bf16[32,16,128]{2,1,0:T(8,128)(2,1)}), bf16[32,16,128]{2,1,0:T(8,128)(2,1)S(1)}, u32[]{:S(2)}, u32[]{:S(2)}) async-start(bf16[32,16,128]{2,1,0:T(8,128)(2,1)} %broadcast_in_dim.22), calls=%async_computation.2 | async-start | bytes 262144 | tf_op jit(solution)/shard_map/all_to_all | solution.py:244
  81.7 0.0 collective-permute-done.4.act_ref
  81.7 0.0 collective-permute-done.5.row_ref
  81.7 1.7 %shard_map.79 = (bf16[64,2,8,128]{3,2,1,0:T(8,128)(2,1)}, bf16[32,2,8,128]{3,2,1,0:T(8,128)(2,1)}) custom-call(s32[1]{0:T(128)} %bitcast.sy_ref, bf16[2,8,64,128]{3,2,1,0:T(8,128)(2,1)S(1)} %collective-permute-done.3.got_ref, bf16[8,64,128]{2,1,0:T(8,128)(2,1)S(1)} %collective-permute-done.4.act_ref, bf16[2,8,64,128]{3,2,1,0:T(8,128)(2,1)S(1)} %get-tuple-element.34.send_ref, ...), custom_call_target="tpu_custom_call" | custom-call | flops 4000000000 | bytes 1048576 | tf_op jit(solution)/shard_map/pallas_call | solution.py:33
  83.4 7.9 %all-to-all-done.2 = bf16[32,16,128]{2,1,0:T(8,128)(2,1)S(1)} async-done(((bf16[32,16,128]{2,1,0:T(8,128)(2,1)}), bf16[32,16,128]{2,1,0:T(8,128)(2,1)S(1)}, u32[]{:S(2)}, u32[]{:S(2)}) %all-to-all-start.2) | async-done | bytes 131104 | tf_op jit(solution)/shard_map/all_to_all | solution.py:244
  91.4 0.9 shard_map.80
  (6 shorter events, 0.1 us)
Async XLA Ops:
  0.6 2.4 %copy-start = (bf16[1,64,2,8,128]{4,3,2,1,0:T(8,128)(2,1)S(1)}, bf16[1,64,2,8,128]{4,3,2,1,0:T(8,128)(2,1)}, u32[]{:S(2)}) copy-start(bf16[1,64,2,8,128]{4,3,2,1,0:T(8,128)(2,1)} %param.7) | copy-start | bytes 786436
  0.6 0.9 %copy-start.2 = (bf16[1,32,2,8,128]{4,3,2,1,0:T(8,128)(2,1)S(1)}, bf16[1,32,2,8,128]{4,3,2,1,0:T(8,128)(2,1)}, u32[]{:S(2)}) copy-start(bf16[1,32,2,8,128]{4,3,2,1,0:T(8,128)(2,1)} %param.4) | copy-start | bytes 393220
  1.7 7.8 %collective-permute-start = (bf16[2,8,32,128]{3,2,1,0:T(8,128)(2,1)S(1)}, bf16[2,8,32,128]{3,2,1,0:T(8,128)(2,1)S(1)}, u32[]{:S(2)}, u32[]{:S(2)}) collective-permute-start(bf16[2,8,32,128]{3,2,1,0:T(8,128)(2,1)S(1)} %get-tuple-element.24.own_ref), channel_id=1, source_target_pairs={{2,0},{4,2},{6,4},{8,6},{10,8},{3,1},{5,3},{7,5},{9,7},{11,9},{14,... | collective-permute-start | bytes 393224 | tf_op jit(solution)/shard_map/ppermute | solution.py:279
  3.0 0.7 copy-start.3
  3.6 0.9 %copy-start.1 = (bf16[64,32,3,3,3]{0,1,4,3,2:T(8,128)(2,1)S(1)}, bf16[64,32,3,3,3]{0,1,4,3,2:T(8,128)(2,1)}, u32[]{:S(2)}) copy-start(bf16[64,32,3,3,3]{0,1,4,3,2:T(8,128)(2,1)} %param.5) | copy-start | bytes 331780
  4.9 19.4 %collective-permute-start.2 = (bf16[8,64,128]{2,1,0:T(8,128)(2,1)S(1)}, bf16[8,64,128]{2,1,0:T(8,128)(2,1)S(1)}, u32[]{:S(2)}, u32[]{:S(2)}) collective-permute-start(bf16[8,64,128]{2,1,0:T(8,128)(2,1)S(1)} %get-tuple-element.27.lo_ref), channel_id=1, source_target_pairs={{2,0},{4,2},{6,4},{8,6},{10,8},{3,1},{5,3},{7,5},{9,7},{11,9},{14,... | collective-permute-start | bytes 393224 | tf_op jit(solution)/shard_map/ppermute | solution.py:288
  9.5 17.2 %collective-permute-start.1 = (bf16[4,32,128]{2,1,0:T(8,128)(2,1)S(1)}, bf16[4,32,128]{2,1,0:T(8,128)(2,1)S(1)}, u32[]{:S(2)}, u32[]{:S(2)}) collective-permute-start(bf16[4,32,128]{2,1,0:T(8,128)(2,1)S(1)} %pad_maximum_fusion), channel_id=1, source_target_pairs={{0,1},{1,0},{2,3},{3,2},{4,5},{5,4},{6,7},{7,6},{8,9},{9,8},{10,11... | collective-permute-start | bytes 98312 | tf_op jit(solution)/shard_map/ppermute | solution.py:290
  28.7 35.3 %collective-permute-start.3 = (bf16[2,8,64,128]{3,2,1,0:T(8,128)(2,1)S(1)}, bf16[2,8,64,128]{3,2,1,0:T(8,128)(2,1)S(1)}, u32[]{:S(2)}, u32[]{:S(2)}) collective-permute-start(bf16[2,8,64,128]{3,2,1,0:T(8,128)(2,1)S(1)} %get-tuple-element.34.send_ref), channel_id=1, source_target_pairs={{0,2},{2,4},{4,6},{6,8},{8,10},{1,3},{3,5},{5,7},{7,9},{9,11},{12,... | collective-permute-start | bytes 786440 | tf_op jit(solution)/shard_map/ppermute | solution.py:300
  32.9 19.7 %all-to-all-start = ((bf16[32,16,128]{2,1,0:T(8,128)(2,1)}), bf16[32,16,128]{2,1,0:T(8,128)(2,1)S(1)}, u32[]{:S(2)}, u32[]{:S(2)}) async-start(bf16[32,16,128]{2,1,0:T(8,128)(2,1)} %bitcast.11), calls=%async_computation | async-start | bytes 262144 | tf_op jit(solution)/shard_map/all_to_all | solution.py:244
  43.1 38.6 %collective-permute-start.4 = (bf16[8,64,128]{2,1,0:T(8,128)(2,1)S(1)}, bf16[8,64,128]{2,1,0:T(8,128)(2,1)S(1)}, u32[]{:S(2)}, u32[]{:S(2)}) collective-permute-start(bf16[8,64,128]{2,1,0:T(8,128)(2,1)S(1)} %get-tuple-element.35), channel_id=1, source_target_pairs={{0,2},{2,4},{4,6},{6,8},{8,10},{1,3},{3,5},{5,7},{7,9},{9,11},{12,... | collective-permute-start | bytes 393224 | tf_op jit(solution)/shard_map/ppermute | solution.py:305
  53.4 22.9 %all-to-all-start.1 = ((bf16[24,16,128]{2,1,0:T(8,128)(2,1)}), bf16[24,16,128]{2,1,0:T(8,128)(2,1)S(1)}, u32[]{:S(2)}, u32[]{:S(2)}) async-start(bf16[24,16,128]{2,1,0:T(8,128)(2,1)} %broadcast_in_dim.10), calls=%async_computation.1 | async-start | bytes 196608 | tf_op jit(solution)/shard_map/all_to_all | solution.py:244
  64.0 17.7 %collective-permute-start.5 = (bf16[4,64,128]{2,1,0:T(8,128)(2,1)S(1)}, bf16[4,64,128]{2,1,0:T(8,128)(2,1)S(1)}, u32[]{:S(2)}, u32[]{:S(2)}) collective-permute-start(bf16[4,64,128]{2,1,0:T(8,128)(2,1)S(1)} %pad_add_fusion), channel_id=1, source_target_pairs={{0,1},{1,0},{2,3},{3,2},{4,5},{5,4},{6,7},{7,6},{8,9},{9,8},{10,11... | collective-permute-start | bytes 196616 | tf_op jit(solution)/shard_map/ppermute | solution.py:304
  77.0 14.4 %all-to-all-start.2 = ((bf16[32,16,128]{2,1,0:T(8,128)(2,1)}), bf16[32,16,128]{2,1,0:T(8,128)(2,1)S(1)}, u32[]{:S(2)}, u32[]{:S(2)}) async-start(bf16[32,16,128]{2,1,0:T(8,128)(2,1)} %broadcast_in_dim.22), calls=%async_computation.2 | async-start | bytes 262144 | tf_op jit(solution)/shard_map/all_to_all | solution.py:244

commit v5 on v3

--- a/solution.py
+++ b/solution.py
@@ -10,7 +10,7 @@
 BF = jnp.bfloat16
 F32 = jnp.float32
 CI, CO, NX, NY, NZ = 32, 64, 2, 8, 128
-GROUP = ("core", "sx", "sy")
+GROUP = ("sx", "sy")
 SAMP = ("plane", "core")
 NT_DIMS = (((1,), (1,)), ((), ()))
 VM = pl.BlockSpec(memory_space=pltpu.VMEM)
@@ -252,12 +252,12 @@
 
 
 def reduced(part):
-    shares = lax.axis_size("plane")
-    share = everywhere(part.reshape(shares, ROWS // shares, NZ), "plane")
+    shares = lax.axis_size(SAMP)
+    share = everywhere(part.reshape(shares, ROWS // shares, NZ), SAMP)
     share = total(share)
     share = copies(share, GROUP)
     share = total(share)
-    share = copies(share, "plane")
+    share = copies(share, SAMP)
     return share.reshape(ROWS, NZ)
 
 
@@ -312,7 +312,7 @@
         ],
         6, 1, 4 * 10**9,
     )(sy, got, send, keep, swapped, bwd)
-    whole = lax.axis_size("plane") * lax.axis_size(GROUP) * NX * NY * NZ
+    whole = lax.axis_size(SAMP) * lax.axis_size(GROUP) * NX * NY * NZ
     norm = (1.0 / jnp.sqrt(jnp.float32(whole))).reshape(1)
     w, b = call(finish, (o((27 * CI, CO), F32), o((1, CO), F32)), (), 2, 1, 10**8)(norm, summed)
     wgrad = jnp.transpose(w.reshape(3, 3, 3, CI, CO), (4, 3, 0, 1, 2))

time: 91.9 us -> 94 us (1.023)
  the two profiles are of different devices: /device:TPU:8 before, /device:TPU:1 now
where the time goes in v5:
time: 94 us; the launch traced here: 93.6 us
  starting transfers between devices  46.7 us (50%)
  blocking collectives  23.1 us (25%)
  waiting for transfers between devices  12.3 us (13%)
  Pallas kernels  6.68 us (7%)
  local copies, waits for them, and re-layouts  3.84 us (4%)
    all_to_all x1, blocking collectives, everywhere(): return lax.all_to_all(blocks, axis, 0, 0, tiled=True)  23.1 us
    ppermute x1, starting transfers between devices, per_device(): swapped = lax.ppermute(jnp.concatenate([row, edges], axis=0), 'sy', swap)  15.4 us
    all_to_all x2, starting transfers between devices, everywhere(): return lax.all_to_all(blocks, axis, 0, 0, tiled=True)  15.4 us
    ppermute x1, starting transfers between devices, per_device(): swapped = lax.ppermute(edges, 'sy', swap)  9.64 us
    all_to_all x2, waiting for transfers between devices, everywhere(): return lax.all_to_all(blocks, axis, 0, 0, tiled=True)  9.64 us
    pallas_call x6, Pallas kernels, run(): return inner(*args[:smem], *near)  6.68 us
    ppermute x1, starting transfers between devices, per_device(): got = lax.ppermute(send, 'sx', up_line)  3.71 us
    ppermute x1, waiting for transfers between devices, per_device(): after = lax.ppermute(own, 'sx', down_line)  2.62 us
  transfers between devices with their start and end apart: 7, of which 2 were waited for; matrix products, arithmetic and copies ran while one was open for 2% of the time, Pallas kernels for 5%

profile of v5, /device:TPU:1, one launch (start us, length us, event | category | flops | bytes accessed | tf_op | source)
XLA Modules:
  0.0 93.6 jit_solution(11269796505600482579)
XLA Ops:
  0.6 0.0 copy-start
  0.6 0.0 copy-start.2
  0.7 0.9 %copy-done.2 = bf16[1,32,2,8,128]{4,3,2,1,0:T(8,128)(2,1)S(1)} copy-done((bf16[1,32,2,8,128]{4,3,2,1,0:T(8,128)(2,1)S(1)}, bf16[1,32,2,8,128]{4,3,2,1,0:T(8,128)(2,1)}, u32[]{:S(2)}) %copy-start.2) | copy-done | bytes 131096
  1.6 0.1 shard_map.75
  1.7 1.3 %collective-permute-start = (bf16[2,8,32,128]{3,2,1,0:T(8,128)(2,1)S(1)}, bf16[2,8,32,128]{3,2,1,0:T(8,128)(2,1)S(1)}, u32[]{:S(2)}, u32[]{:S(2)}) collective-permute-start(bf16[2,8,32,128]{3,2,1,0:T(8,128)(2,1)S(1)} %get-tuple-element.22.own_ref), channel_id=1, source_target_pairs={{2,0},{4,2},{6,4},{8,6},{10,8},{3,1},{5,3},{7,5},{9,7},{11,9},{14,... | collective-permute-start | bytes 393224 | tf_op jit(solution)/shard_map/ppermute | solution.py:278
  3.0 0.0 copy-start.3
  3.0 0.0 copy-done
  3.0 0.6 copy-done.3
  3.6 0.0 copy-start.1
  3.7 0.9 copy-done.1
  4.6 0.3 shard_map.76
  4.9 1.3 %collective-permute-start.2 = (bf16[8,64,128]{2,1,0:T(8,128)(2,1)S(1)}, bf16[8,64,128]{2,1,0:T(8,128)(2,1)S(1)}, u32[]{:S(2)}, u32[]{:S(2)}) collective-permute-start(bf16[8,64,128]{2,1,0:T(8,128)(2,1)S(1)} %get-tuple-element.25.lo_ref), channel_id=1, source_target_pairs={{2,0},{4,2},{6,4},{8,6},{10,8},{3,1},{5,3},{7,5},{9,7},{11,9},{14,... | collective-permute-start | bytes 393224 | tf_op jit(solution)/shard_map/ppermute | solution.py:287
  6.2 2.6 %collective-permute-done.next_ref = bf16[2,8,32,128]{3,2,1,0:T(8,128)(2,1)S(1)} collective-permute-done((bf16[2,8,32,128]{3,2,1,0:T(8,128)(2,1)S(1)}, bf16[2,8,32,128]{3,2,1,0:T(8,128)(2,1)S(1)}, u32[]{:S(2)}, u32[]{:S(2)}) %collective-permute-start) | collective-permute-done | bytes 131104 | tf_op jit(solution)/shard_map/ppermute | solution.py:278
  8.9 15.4 %collective-permute-start.1 = (bf16[4,32,128]{2,1,0:T(8,128)(2,1)S(1)}, bf16[4,32,128]{2,1,0:T(8,128)(2,1)S(1)}, u32[]{:S(2)}, u32[]{:S(2)}) collective-permute-start(bf16[4,32,128]{2,1,0:T(8,128)(2,1)S(1)} %pad_maximum_fusion), channel_id=1, source_target_pairs={{0,1},{1,0},{2,3},{3,2},{4,5},{5,4},{6,7},{7,6},{8,9},{9,8},{10,11... | collective-permute-start | bytes 98312 | tf_op jit(solution)/shard_map/ppermute | solution.py:289
  24.3 0.0 collective-permute-done.2.up_ref
  24.3 2.3 %shard_map.77 = (bf16[3,8,64,128]{3,2,1,0:T(8,128)(2,1)S(1)}, bf16[3,8,64,128]{3,2,1,0:T(8,128)(2,1)S(1)}, f32[304,256]{1,0:T(8,128)S(1)}) custom-call(s32[1]{0:T(128)} %bitcast.sy_ref, s32[1]{0:T(128)} %bitcast.1.sx_ref, bf16[2,8,32,128]{3,2,1,0:T(8,128)(2,1)S(1)} %get-tuple-element.22.own_ref, bf16[2,8,32,128]{3,2,1,0:T(8,128)(2,1)S(1)} %collective-permute-done.next_ref, ...), custom_call_target="tpu_custom_call" | custom-call | flops 3000000000 | bytes 1048576 | tf_op jit(solution)/shard_map/pallas_call | solution.py:33
  26.6 0.0 collective-permute-done.1.row_ref
  26.6 1.3 %shard_map.78 = (bf16[3,8,64,128]{3,2,1,0:T(8,128)(2,1)S(1)}, bf16[3,8,64,128]{3,2,1,0:T(8,128)(2,1)S(1)}, bf16[4,64,128]{2,1,0:T(8,128)(2,1)S(1)}, bf16[512,128]{1,0:T(8,128)(2,1)S(1)}) custom-call(s32[1]{0:T(128)} %bitcast.sy_ref, s32[1]{0:T(128)} %bitcast.1.sx_ref, bf16[2,8,32,128]{3,2,1,0:T(8,128)(2,1)S(1)} %get-tuple-element.22.own_ref, ...), custom_call_target="tpu_custom_call" | custom-call | flops 1000000000 | bytes 1048576 | tf_op jit(solution)/shard_map/pallas_call | solution.py:33
  28.0 3.7 %collective-permute-start.3 = (bf16[3,8,64,128]{3,2,1,0:T(8,128)(2,1)S(1)}, bf16[3,8,64,128]{3,2,1,0:T(8,128)(2,1)S(1)}, u32[]{:S(2)}, u32[]{:S(2)}) collective-permute-start(bf16[3,8,64,128]{3,2,1,0:T(8,128)(2,1)S(1)} %get-tuple-element.31.send_ref), channel_id=1, source_target_pairs={{0,2},{2,4},{4,6},{6,8},{8,10},{1,3},{3,5},{5,7},{7,9},{9,11},{12,... | collective-permute-start | bytes 1179656 | tf_op jit(solution)/shard_map/ppermute | solution.py:299
  31.7 23.1 %all_to_all.15 = bf16[64,8,128]{2,1,0:T(8,128)(2,1)S(1)} all-to-all(bf16[64,8,128]{2,1,0:T(8,128)(2,1)S(1)} %bitcast.21), channel_id=1, replica_groups=mesh['plane'=32,'core'=2,'sx'=6,'sy'=2] {'plane','core'}, dimensions={0} | all-to-all | bytes 262144 | tf_op jit(solution)/shard_map/all_to_all | solution.py:243
  54.8 0.1 reduce_sum.24
  54.9 0.6 broadcast_in_dim.10
  55.5 10.1 %all-to-all-start.1 = ((bf16[12,8,128]{2,1,0:T(8,128)(2,1)}), bf16[12,8,128]{2,1,0:T(8,128)(2,1)S(1)}, u32[]{:S(2)}, u32[]{:S(2)}) async-start(bf16[12,8,128]{2,1,0:T(8,128)(2,1)} %broadcast_in_dim.10), calls=%async_computation.1 | async-start | bytes 49152 | tf_op jit(solution)/shard_map/all_to_all | solution.py:243
  65.6 0.0 collective-permute-done.3.got_ref
  65.7 9.6 %collective-permute-start.4 = (bf16[4,64,128]{2,1,0:T(8,128)(2,1)S(1)}, bf16[4,64,128]{2,1,0:T(8,128)(2,1)S(1)}, u32[]{:S(2)}, u32[]{:S(2)}) collective-permute-start(bf16[4,64,128]{2,1,0:T(8,128)(2,1)S(1)} %pad_add_fusion), channel_id=1, source_target_pairs={{0,1},{1,0},{2,3},{3,2},{4,5},{5,4},{6,7},{7,6},{8,9},{9,8},{10,11... | collective-permute-start | bytes 196616 | tf_op jit(solution)/shard_map/ppermute | solution.py:303
  75.3 0.0 all-to-all-done.1
  75.4 0.7 broadcast_in_dim.22
  76.0 5.3 %all-to-all-start.2 = ((bf16[64,8,128]{2,1,0:T(8,128)(2,1)}), bf16[64,8,128]{2,1,0:T(8,128)(2,1)S(1)}, u32[]{:S(2)}, u32[]{:S(2)}) async-start(bf16[64,8,128]{2,1,0:T(8,128)(2,1)} %broadcast_in_dim.22), calls=%async_computation.2 | async-start | bytes 262144 | tf_op jit(solution)/shard_map/all_to_all | solution.py:243
  81.3 0.0 collective-permute-done.4.row_ref
  81.3 1.7 %shard_map.79 = (bf16[64,2,8,128]{3,2,1,0:T(8,128)(2,1)}, bf16[32,2,8,128]{3,2,1,0:T(8,128)(2,1)}) custom-call(s32[1]{0:T(128)} %bitcast.sy_ref, bf16[3,8,64,128]{3,2,1,0:T(8,128)(2,1)S(1)} %collective-permute-done.3.got_ref, bf16[3,8,64,128]{3,2,1,0:T(8,128)(2,1)S(1)} %get-tuple-element.31.send_ref, bf16[3,8,64,128]{3,2,1,0:T(8,128)(2,1)S(1)} %get-tuple-element.32.keep_ref, ...), custom_call_target="tpu_custom_call" | custom-call | flops 4000000000 | bytes 1048576 | tf_op jit(solution)/shard_map/pallas_call | solution.py:33
  83.0 9.6 %all-to-all-done.2 = bf16[64,8,128]{2,1,0:T(8,128)(2,1)S(1)} async-done(((bf16[64,8,128]{2,1,0:T(8,128)(2,1)}), bf16[64,8,128]{2,1,0:T(8,128)(2,1)S(1)}, u32[]{:S(2)}, u32[]{:S(2)}) %all-to-all-start.2) | async-done | bytes 131104 | tf_op jit(solution)/shard_map/all_to_all | solution.py:243
  92.7 0.9 shard_map.80
  (6 shorter events, 0.1 us)
Async XLA Ops:
  0.6 2.4 %copy-start = (bf16[1,64,2,8,128]{4,3,2,1,0:T(8,128)(2,1)S(1)}, bf16[1,64,2,8,128]{4,3,2,1,0:T(8,128)(2,1)}, u32[]{:S(2)}) copy-start(bf16[1,64,2,8,128]{4,3,2,1,0:T(8,128)(2,1)} %param.7) | copy-start | bytes 786436
  0.6 0.9 %copy-start.2 = (bf16[1,32,2,8,128]{4,3,2,1,0:T(8,128)(2,1)S(1)}, bf16[1,32,2,8,128]{4,3,2,1,0:T(8,128)(2,1)}, u32[]{:S(2)}) copy-start(bf16[1,32,2,8,128]{4,3,2,1,0:T(8,128)(2,1)} %param.4) | copy-start | bytes 393220
  1.7 7.2 %collective-permute-start = (bf16[2,8,32,128]{3,2,1,0:T(8,128)(2,1)S(1)}, bf16[2,8,32,128]{3,2,1,0:T(8,128)(2,1)S(1)}, u32[]{:S(2)}, u32[]{:S(2)}) collective-permute-start(bf16[2,8,32,128]{3,2,1,0:T(8,128)(2,1)S(1)} %get-tuple-element.22.own_ref), channel_id=1, source_target_pairs={{2,0},{4,2},{6,4},{8,6},{10,8},{3,1},{5,3},{7,5},{9,7},{11,9},{14,... | collective-permute-start | bytes 393224 | tf_op jit(solution)/shard_map/ppermute | solution.py:278
  3.0 0.7 copy-start.3
  3.6 0.9 %copy-start.1 = (bf16[64,32,3,3,3]{0,1,4,3,2:T(8,128)(2,1)S(1)}, bf16[64,32,3,3,3]{0,1,4,3,2:T(8,128)(2,1)}, u32[]{:S(2)}) copy-start(bf16[64,32,3,3,3]{0,1,4,3,2:T(8,128)(2,1)} %param.5) | copy-start | bytes 331780
  4.9 19.4 %collective-permute-start.2 = (bf16[8,64,128]{2,1,0:T(8,128)(2,1)S(1)}, bf16[8,64,128]{2,1,0:T(8,128)(2,1)S(1)}, u32[]{:S(2)}, u32[]{:S(2)}) collective-permute-start(bf16[8,64,128]{2,1,0:T(8,128)(2,1)S(1)} %get-tuple-element.25.lo_ref), channel_id=1, source_target_pairs={{2,0},{4,2},{6,4},{8,6},{10,8},{3,1},{5,3},{7,5},{9,7},{11,9},{14,... | collective-permute-start | bytes 393224 | tf_op jit(solution)/shard_map/ppermute | solution.py:287
  8.9 17.8 %collective-permute-start.1 = (bf16[4,32,128]{2,1,0:T(8,128)(2,1)S(1)}, bf16[4,32,128]{2,1,0:T(8,128)(2,1)S(1)}, u32[]{:S(2)}, u32[]{:S(2)}) collective-permute-start(bf16[4,32,128]{2,1,0:T(8,128)(2,1)S(1)} %pad_maximum_fusion), channel_id=1, source_target_pairs={{0,1},{1,0},{2,3},{3,2},{4,5},{5,4},{6,7},{7,6},{8,9},{9,8},{10,11... | collective-permute-start | bytes 98312 | tf_op jit(solution)/shard_map/ppermute | solution.py:289
  28.0 37.6 %collective-permute-start.3 = (bf16[3,8,64,128]{3,2,1,0:T(8,128)(2,1)S(1)}, bf16[3,8,64,128]{3,2,1,0:T(8,128)(2,1)S(1)}, u32[]{:S(2)}, u32[]{:S(2)}) collective-permute-start(bf16[3,8,64,128]{3,2,1,0:T(8,128)(2,1)S(1)} %get-tuple-element.31.send_ref), channel_id=1, source_target_pairs={{0,2},{2,4},{4,6},{6,8},{8,10},{1,3},{3,5},{5,7},{7,9},{9,11},{12,... | collective-permute-start | bytes 1179656 | tf_op jit(solution)/shard_map/ppermute | solution.py:299
  55.5 19.8 %all-to-all-start.1 = ((bf16[12,8,128]{2,1,0:T(8,128)(2,1)}), bf16[12,8,128]{2,1,0:T(8,128)(2,1)S(1)}, u32[]{:S(2)}, u32[]{:S(2)}) async-start(bf16[12,8,128]{2,1,0:T(8,128)(2,1)} %broadcast_in_dim.10), calls=%async_computation.1 | async-start | bytes 49152 | tf_op jit(solution)/shard_map/all_to_all | solution.py:243
  65.7 15.7 %collective-permute-start.4 = (bf16[4,64,128]{2,1,0:T(8,128)(2,1)S(1)}, bf16[4,64,128]{2,1,0:T(8,128)(2,1)S(1)}, u32[]{:S(2)}, u32[]{:S(2)}) collective-permute-start(bf16[4,64,128]{2,1,0:T(8,128)(2,1)S(1)} %pad_add_fusion), channel_id=1, source_target_pairs={{0,1},{1,0},{2,3},{3,2},{4,5},{5,4},{6,7},{7,6},{8,9},{9,8},{10,11... | collective-permute-start | bytes 196616 | tf_op jit(solution)/shard_map/ppermute | solution.py:303
  76.0 16.6 %all-to-all-start.2 = ((bf16[64,8,128]{2,1,0:T(8,128)(2,1)}), bf16[64,8,128]{2,1,0:T(8,128)(2,1)S(1)}, u32[]{:S(2)}, u32[]{:S(2)}) async-start(bf16[64,8,128]{2,1,0:T(8,128)(2,1)} %broadcast_in_dim.22), calls=%async_computation.2 | async-start | bytes 262144 | tf_op jit(solution)/shard_map/all_to_all | solution.py:243
